TPU v7x, 128 devices: a whole 4x4x4 slice. The times are simulated.
128 devices in a mesh: data: 128 (over z, y, x, core).
Axes of the slice: x: 4, y: 4, z: 4, core: 2. Of those that a mesh axis runs over, the one named last changes fastest.
Arguments:
- act_in: bfloat16 [131072, 768], P('data')
- grad_out: bfloat16 [131072, 768], P('data')
- w_up1: bfloat16 [768, 3072], replicated
- w_down1: bfloat16 [3072, 768], replicated
- w_up2: bfloat16 [768, 3072], replicated
- w_down2: bfloat16 [3072, 768], replicated
- master_up1: float32 [768, 3072], P('data')
- master_down1: float32 [3072, 768], P('data')
- master_up2: float32 [768, 3072], P('data')
- master_down2: float32 [3072, 768], P('data')
- mom_up1: float32 [768, 3072], P('data')
- mom_down1: float32 [3072, 768], P('data')
- mom_up2: float32 [768, 3072], P('data')
- mom_down2: float32 [3072, 768], P('data')
- vel_up1: float32 [768, 3072], P('data')
- vel_down1: float32 [3072, 768], P('data')
- vel_up2: float32 [768, 3072], P('data')
- vel_down2: float32 [3072, 768], P('data')
- learn_rate: float32 [], replicated
- clip_norm: float32 [], replicated
Outputs:
- output 1: bfloat16 [768, 3072], replicated
- output 2: bfloat16 [3072, 768], replicated
- output 3: bfloat16 [768, 3072], replicated
- output 4: bfloat16 [3072, 768], replicated
- output 5: float32 [768, 3072], P('data')
- output 6: float32 [3072, 768], P('data')
- output 7: float32 [768, 3072], P('data')
- output 8: float32 [3072, 768], P('data')
- output 9: float32 [768, 3072], P('data')
- output 10: float32 [3072, 768], P('data')
- output 11: float32 [768, 3072], P('data')
- output 12: float32 [3072, 768], P('data')
- output 13: float32 [768, 3072], P('data')
- output 14: float32 [3072, 768], P('data')
- output 15: float32 [768, 3072], P('data')
- output 16: float32 [3072, 768], P('data')
- output 17: float32 [], replicated
All inputs are finite; a program needn't handle non-finite values.
Results may differ from a plain program's by a relative error of at most 0.0109451.
Values are sent between devices in bfloat16 or wider.
A program may use at most 1 GiB of HBM per device.

v0:
```python
import functools
import math
import jax
import jax.numpy as jnp
from jax import lax
from jax.experimental import pallas as pl
from jax.experimental.pallas import tpu as pltpu
from jax.sharding import PartitionSpec as P

STEP = 20
BETA_ONE = 0.9
BETA_TWO = 0.95
EPSILON = 1e-8
NORM_EPS = 1e-6
CORR_ONE = 1.0 - BETA_ONE ** STEP
CORR_TWO = 1.0 - BETA_TWO ** STEP
ROOT_HALF = math.sqrt(0.5)
INV_ROOT_TAU = 1.0 / math.sqrt(2.0 * math.pi)

MESH = pl.DeviceIdType.MESH
STRIDES = (32, 8, 2)
ORDERS = ((2, 1, 0), (1, 0, 2), (0, 2, 1))
ROWS = 24
SUB = 6
CHUNK = 8


def adam_step(scaled, master_old, mom_old, vel_old, learn_rate):
    mom_new = BETA_ONE * mom_old + (1.0 - BETA_ONE) * scaled
    vel_new = BETA_TWO * vel_old + (1.0 - BETA_TWO) * scaled * scaled
    master_new = master_old - learn_rate * (mom_new / CORR_ONE) / (jnp.sqrt(vel_new / CORR_TWO) + EPSILON)
    return master_new, mom_new, vel_new


def comm_kernel(lanes, *refs):
    (g_up1, g_down1, g_up2, g_down2), refs = refs[:4], refs[4:]
    states, refs = refs[:12], refs[12:]
    (lr_ref, clip_ref), refs = refs[:2], refs[2:]
    (w_out, up_out, down_out, norm_out), refs = refs[:4], refs[4:]
    (total, peer_in, rs1, rs2, rs3, norm_core, norm_axis, send_g, recv_g, send_w, recv_w, block_tmp, w_own, up_state, down_state), refs = refs[:15], refs[15:]
    (load_sem, state_sem, pair_s, pair_r, rs1_s, rs1_r, rs2_s, rs2_r, rs3_s, rs3_r, nc_s, nc_r, na_s, na_r, xg_s, xg_r, xw_s, xw_r, own_sem, ag_s, ag_r, out_s, out_r) = refs
    half = lanes // 2
    me = lax.axis_index("data")
    core = lax.rem(me, 2)
    member = lax.rem(me, 4)
    pos = (me // 32, lax.rem(me // 8, 4), lax.rem(me // 2, 4))
    partner = me + 1 - 2 * core

    def device(axis, coord):
        return me + (coord - pos[axis]) * STRIDES[axis]

    def step(axis, hops):
        return lax.rem(pos[axis] + hops, 4)

    def remote(src, dst, send_sem, recv_sem, target):
        return pltpu.make_async_remote_copy(src_ref=src, dst_ref=dst, send_sem=send_sem, recv_sem=recv_sem, device_id=(target,), device_id_type=MESH)

    peers = [partner] + [device(axis, step(axis, hops)) for axis in range(3) for hops in (1, 2, 3)]
    peers.append(me - member + lax.rem(member + 2, 4) + 1 - 2 * core)
    barrier = pltpu.get_barrier_semaphore()
    for peer in peers:
        pl.semaphore_signal(barrier, inc=1, device_id=(peer,), device_id_type=MESH)

    grads = (g_up1, g_down1, g_up2, g_down2)
    mat_order = (3, 2, 1, 0)

    def pieces(mat, owner):
        if mat % 2:
            return [(grads[mat].at[:, :, :, owner], (mat,))]
        out = []
        for x in range(4):
            col = pl.multiple_of(((x % 2) * 2 + owner) * lanes, lanes)
            out.append((grads[mat].at[:, :, x // 2, :, pl.ds(col, lanes)], (mat, slice(None), slice(None), x)))
        return out

    loads, pairs = {}, {}
    for mat in mat_order:
        loads[mat] = [pltpu.make_async_copy(src, total.at[dst], load_sem.at[mat, i]) for i, (src, dst) in enumerate(pieces(mat, core))]
        for copy in loads[mat]:
            copy.start()
    state_loads = []
    for field in range(3):
        for mat in range(4):
            dst = (down_state if mat % 2 else up_state).at[field, mat // 2]
            copy = pltpu.make_async_copy(states[4 * field + mat], dst, state_sem.at[field, mat])
            copy.start()
            state_loads.append(copy)
    pl.semaphore_wait(barrier, len(peers))
    for mat in mat_order:
        pairs[mat] = [remote(src, peer_in.at[dst], pair_s.at[mat, i], pair_r.at[mat, i], partner) for i, (src, dst) in enumerate(pieces(mat, 1 - core))]
        for copy in pairs[mat]:
            copy.start()

    def part(mats, coords, colour, side):
        index = [mats, slice(None), slice(None), slice(None), pl.ds(CHUNK * colour, CHUNK), pl.ds(half * side, half)]
        for axis, coord in coords.items():
            index[1 + axis] = coord
        return tuple(index)

    class Phase:
        def __init__(self, level, mats, buf, send_sem, recv_sem):
            self.level, self.mats, self.buf, self.send_sem, self.recv_sem = level, mats, buf, send_sem, recv_sem
            self.copies = {}

        def where(self, colour, coord):
            order = ORDERS[colour]
            coords = {axis: pos[axis] for axis in order[:self.level]}
            coords[order[self.level]] = coord
            return coords

        def row(self, colour, coord, side, i):
            coords = self.where(colour, coord)
            if self.level:
                return part(i, coords, colour, side)
            coords[min(axis for axis in range(3) if axis not in coords)] = i
            return part(self.mats, coords, colour, side)

        def send(self, colour, side, kind, src, target):
            copy = remote(src, self.buf.at[colour, side, kind], self.send_sem.at[colour, side, kind], self.recv_sem.at[colour, side, kind], target)
            copy.start()
            self.copies[colour, side, kind] = copy

        def near(self, colour, side):
            axis = ORDERS[colour][self.level]
            coord = step(axis, 1 if side == 0 else 3)
            return coord, device(axis, coord)

        def start(self):
            for kind in range(2):
                for colour in range(3):
                    for side in range(2):
                        coord, target = self.near(colour, side)
                        aim = step(ORDERS[colour][self.level], 2) if kind == 0 else coord
                        src = total.at[part(self.mats, self.where(colour, aim), colour, side if kind == 0 else 1 - side)]
                        self.send(colour, side, kind, src, target)

        def forward(self):
            for colour in range(3):
                for side in range(2):
                    coord, target = self.near(colour, side)
                    self.copies[colour, side, 0].wait_recv()

                    def add_own(i, carry, colour=colour, side=side, coord=coord):
                        self.buf[colour, side, 0, i] = self.buf[colour, side, 0, i] + total[self.row(colour, coord, side, i)]
                        return carry

                    lax.fori_loop(0, 4, add_own, 0)
                    self.send(colour, side, 2, self.buf.at[colour, side, 0], target)

        def finish(self):
            for colour in range(3):
                for side in range(2):
                    self.copies[colour, 1 - side, 1].wait_recv()
                    self.copies[colour, side, 2].wait_recv()

                    def add_both(i, carry, colour=colour, side=side):
                        own = self.row(colour, pos[ORDERS[colour][self.level]], side, i)
                        total[own] = total[own] + (self.buf[colour, 1 - side, 1, i] + self.buf[colour, side, 2, i])
                        return carry

                    lax.fori_loop(0, 4, add_both, 0)

        def drain(self):
            for copy in self.copies.values():
                copy.wait_send()

    everything = slice(None)
    first = {}
    previous = None
    for mat in mat_order:
        for copy in loads[mat]:
            copy.wait()
        for copy in pairs[mat]:
            copy.wait_recv()

        def add_pair(i, carry, mat=mat):
            total[mat, i // 4, lax.rem(i, 4)] = total[mat, i // 4, lax.rem(i, 4)] + peer_in[mat, i // 4, lax.rem(i, 4)]
            return carry

        lax.fori_loop(0, 16, add_pair, 0)
        first[mat] = Phase(0, mat, rs1.at[mat], rs1_s.at[mat], rs1_r.at[mat])
        first[mat].start()
        if previous is not None:
            first[previous].forward()
        previous = mat
    first[previous].forward()
    for mat in mat_order:
        first[mat].finish()
    second = Phase(1, everything, rs2, rs2_s, rs2_r)
    second.start()
    second.forward()
    second.finish()
    third = Phase(2, everything, rs3, rs3_s, rs3_r)
    third.start()
    third.forward()
    third.finish()

    group_scale = 1.0 / 128.0
    grad_own = [total[mat, pos[0], pos[1], pos[2]] * group_scale for mat in range(4)]
    partial = None
    for block in grad_own:
        square = block * block
        for row in range(ROWS // 8):
            for col in range(max(1, lanes // 128)):
                tile = square[8 * row:8 * row + 8, 128 * col:128 * col + 128]
                partial = tile if partial is None else partial + tile
    norm_core[core] = partial
    swap = remote(norm_core.at[core], norm_core.at[core], nc_s.at[0], nc_r.at[0], partner)
    swap.start()
    for target in range(4):
        for i, mat in enumerate((0, 2)):
            send_g[target, i] = grad_own[mat][SUB * target:SUB * target + SUB]
    moves = []
    for hops in range(1, 4):
        other = lax.rem(member + hops, 4)
        copy = remote(send_g.at[other], recv_g.at[member], xg_s.at[hops - 1], xg_r.at[hops - 1], me - member + other)
        copy.start()
        moves.append(copy)
    recv_g[member] = send_g[member]
    swap.wait_recv()
    running = norm_core[0] + norm_core[1]
    sends = [swap] + moves
    for axis in (2, 1, 0):
        norm_axis[axis, pos[axis]] = running
        copies = []
        for hops in (1, 2, 3):
            coord = step(axis, hops)
            copy = remote(norm_axis.at[axis, pos[axis]], norm_axis.at[axis, pos[axis]], na_s.at[axis, hops - 1], na_r.at[axis, hops - 1], device(axis, coord))
            copy.start()
            copies.append(copy)
        for copy in copies:
            copy.wait_recv()
        sends = sends + copies
        running = (norm_axis[axis, 0] + norm_axis[axis, 1]) + (norm_axis[axis, 2] + norm_axis[axis, 3])
    norm = jnp.sqrt(jnp.sum(jnp.sum(running, axis=1, keepdims=True), axis=0, keepdims=True))
    norm_out[...] = jnp.broadcast_to(norm, norm_out.shape)
    clip_scale = jnp.minimum(1.0, clip_ref[0] / (norm + NORM_EPS))
    learn_rate = lr_ref[0]

    for copy in moves:
        copy.wait_recv()
    for copy in state_loads:
        copy.wait()
    for i in range(2):
        for col in range(4):
            cols = slice(col * lanes, (col + 1) * lanes)
            scaled = recv_g[col, i] * clip_scale
            fresh = adam_step(scaled, up_state[0, i, :, cols], up_state[1, i, :, cols], up_state[2, i, :, cols], learn_rate)
            for field in range(3):
                up_state[field, i, :, cols] = fresh[field]
            send_w[col, i] = fresh[0]
    moves = []
    for hops in range(1, 4):
        other = lax.rem(member + hops, 4)
        copy = remote(send_w.at[other], recv_w.at[member], xw_s.at[hops - 1], xw_r.at[hops - 1], me - member + other)
        copy.start()
        moves.append(copy)
    recv_w[member] = send_w[member]
    for mat in (1, 3):
        i = mat // 2
        fresh = adam_step(grad_own[mat] * clip_scale, down_state[0, i], down_state[1, i], down_state[2, i], learn_rate)
        for field in range(3):
            down_state[field, i] = fresh[field]
        w_own[mat] = fresh[0].astype(jnp.bfloat16)
    for copy in moves:
        copy.wait_recv()
    sends = sends + moves
    for i, mat in enumerate((0, 2)):
        for source in range(4):
            block_tmp[SUB * source:SUB * source + SUB] = recv_w[source, i]
        w_own[mat] = block_tmp[...].astype(jnp.bfloat16)

    keep = pltpu.make_async_copy(w_own, w_out.at[:, pos[0], pos[1], pos[2], core], own_sem)
    keep.start()
    state_stores = [pltpu.make_async_copy(up_state, up_out, state_sem.at[0, 0]), pltpu.make_async_copy(down_state, down_out, state_sem.at[0, 1])]
    for copy in state_stores:
        copy.start()

    def spot(coords, colour, side):
        lane = slice(None) if side is None else pl.ds(half * side, half)
        index = [slice(None), slice(None), slice(None), slice(None), core, pl.ds(CHUNK * colour, CHUNK), lane]
        for axis, coord in coords.items():
            index[1 + axis] = coord
        return w_out.at[tuple(index)]

    handed = []

    def hand(ref, slot):
        copy = remote(ref, ref, out_s.at[slot], out_r.at[slot], partner)
        copy.start()
        handed.append(copy)

    for level in (2, 1, 0):
        if level == 1:
            keep.wait()

        def where(colour, coord):
            order = ORDERS[colour]
            coords = {axis: pos[axis] for axis in order[:level]}
            coords[order[level]] = coord
            return coords

        def near(colour, side):
            axis = ORDERS[colour][level]
            coord = step(axis, 1 if side == 0 else 3)
            return coord, device(axis, coord)

        copies = {}
        for kind in range(2):
            for colour in range(3):
                for side in range(2):
                    lane_side = side if kind == 0 else 1 - side
                    dst = spot(where(colour, pos[ORDERS[colour][level]]), colour, lane_side)
                    src = w_own.at[:, pl.ds(CHUNK * colour, CHUNK), pl.ds(half * lane_side, half)] if level == 2 else dst
                    copy = remote(src, dst, ag_s.at[level, colour, side, kind], ag_r.at[level, colour, side, kind], near(colour, side)[1])
                    copy.start()
                    copies[colour, side, kind] = copy
        if level == 0:
            for colour in range(3):
                hand(spot(where(colour, pos[ORDERS[colour][0]]), colour, None), 5 * colour)
        for colour in range(3):
            for side in range(2):
                back = near(colour, 1 - side)[0]
                copies[colour, side, 0].wait_recv()
                ref = spot(where(colour, back), colour, side)
                copy = remote(ref, ref, ag_s.at[level, colour, side, 2], ag_r.at[level, colour, side, 2], near(colour, side)[1])
                copy.start()
                copies[colour, side, 2] = copy
        for colour in range(3):
            for side in range(2):
                copies[colour, side, 1].wait_recv()
                if level == 0:
                    hand(spot(where(colour, near(colour, 1 - side)[0]), colour, None), 5 * colour + 1 + side)
        for colour in range(3):
            for side in range(2):
                copies[colour, side, 2].wait_recv()
                if level == 0:
                    hand(spot(where(colour, step(ORDERS[colour][0], 2)), colour, side), 5 * colour + 3 + side)
        sends = sends + list(copies.values())
    for phase in list(first.values()) + [second, third]:
        phase.drain()
    for mat in mat_order:
        for copy in pairs[mat]:
            copy.wait_send()
    for copy in sends:
        copy.wait_send()
    for copy in handed + state_stores:
        copy.wait()


def place_kernel(lanes, w_ref, up_ref, down_ref, norm_ref, *refs):
    weights, states, norm_out, (w_tmp, up_tmp, down_tmp, in_sem, state_in, out_sem, state_out) = refs[:4], refs[4:16], refs[16], refs[17:]
    norm_out[0] = jnp.max(norm_ref[...])
    loads = [[pltpu.make_async_copy(w_ref.at[mat, z], w_tmp.at[mat, z], in_sem.at[mat, z]) for z in range(4)] for mat in range(4)]
    for row in loads:
        for copy in row:
            copy.start()
    state_loads = [pltpu.make_async_copy(up_ref, up_tmp, state_in.at[0]), pltpu.make_async_copy(down_ref, down_tmp, state_in.at[1])]
    for copy in state_loads:
        copy.start()
    stores = []
    for mat in range(4):
        for z in range(4):
            loads[mat][z].wait()
            if mat % 2:
                copies = [pltpu.make_async_copy(w_tmp.at[mat, z], weights[mat].at[z], out_sem.at[mat, z, 0])]
            else:
                copies = []
                for member in range(4):
                    src = w_tmp.at[mat, z, :, :, member // 2, member % 2]
                    copies.append(pltpu.make_async_copy(src, weights[mat].at[z, :, :, :, pl.ds(member * lanes, lanes)], out_sem.at[mat, z, member]))
            for copy in copies:
                copy.start()
            stores = stores + copies
    for copy in state_loads:
        copy.wait()
    for field in range(3):
        for mat in range(4):
            src = (down_tmp if mat % 2 else up_tmp).at[field, mat // 2]
            copy = pltpu.make_async_copy(src, states[4 * field + mat], state_out.at[field, mat])
            copy.start()
            stores.append(copy)
    for copy in stores:
        copy.wait()


def comm_call(lanes, grads, masters, moms, vels, learn_rate, clip_norm):
    up = (4, 4, 2, ROWS, 4 * lanes)
    down = (4, 4, 4, 2, ROWS, lanes)
    grads = [grads[0].reshape(up), grads[1].reshape(down), grads[2].reshape(up), grads[3].reshape(down)]
    half = lanes // 2
    f32 = jnp.float32
    bf16 = jnp.bfloat16
    up_shape = (3, 2, SUB, 4 * lanes)
    down_shape = (3, 2, ROWS, lanes)
    dma = pltpu.SemaphoreType.DMA
    vmem = pl.BlockSpec(memory_space=pltpu.VMEM)
    smem = pl.BlockSpec(memory_space=pltpu.SMEM)
    hbm = pl.BlockSpec(memory_space=pl.ANY)
    scratch = [
        pltpu.VMEM((4, 4, 4, 4, ROWS, lanes), f32),
        pltpu.VMEM((4, 4, 4, 4, ROWS, lanes), f32),
        pltpu.VMEM((4, 3, 2, 3, 4, 4, CHUNK, half), f32),
        pltpu.VMEM((3, 2, 3, 4, 4, CHUNK, half), f32),
        pltpu.VMEM((3, 2, 3, 4, CHUNK, half), f32),
        pltpu.VMEM((2, 8, min(lanes, 128)), f32),
        pltpu.VMEM((3, 4, 8, min(lanes, 128)), f32),
        pltpu.VMEM((4, 2, SUB, lanes), f32),
        pltpu.VMEM((4, 2, SUB, lanes), f32),
        pltpu.VMEM((4, 2, SUB, lanes), f32),
        pltpu.VMEM((4, 2, SUB, lanes), f32),
        pltpu.VMEM((ROWS, lanes), f32),
        pltpu.VMEM((4, ROWS, lanes), jnp.bfloat16),
        pltpu.VMEM(up_shape, f32),
        pltpu.VMEM(down_shape, f32),
        dma((4, 4)), dma((3, 4)), dma((4, 4)), dma((4, 4)),
        dma((4, 3, 2, 3)), dma((4, 3, 2, 3)), dma((3, 2, 3)), dma((3, 2, 3)), dma((3, 2, 3)), dma((3, 2, 3)),
        dma((1,)), dma((1,)), dma((3, 3)), dma((3, 3)), dma((3,)), dma((3,)), dma((3,)), dma((3,)),
        dma, dma((3, 3, 2, 3)), dma((3, 3, 2, 3)), dma((15,)), dma((15,)),
    ]
    outs = pl.pallas_call(
        functools.partial(comm_kernel, lanes),
        name="reduce_update_gather",
        out_shape=[jax.ShapeDtypeStruct((4, 4, 4, 4, 2, ROWS, lanes), bf16), jax.ShapeDtypeStruct(up_shape, f32), jax.ShapeDtypeStruct(down_shape, f32), jax.ShapeDtypeStruct((8, 128), f32)],
        in_specs=[hbm] * 16 + [smem] * 2,
        out_specs=[hbm] * 3 + [vmem],
        scratch_shapes=scratch,
        compiler_params=pltpu.CompilerParams(collective_id=0, has_side_effects=True, vmem_limit_bytes=67043328),
    )(*grads, *masters, *moms, *vels, learn_rate.reshape(1), clip_norm.reshape(1))
    split = (4, 4, 2, 2, 2, ROWS, lanes)
    placed = pl.pallas_call(
        functools.partial(place_kernel, lanes),
        name="place_outputs",
        out_shape=[jax.ShapeDtypeStruct(split if mat % 2 else up, bf16) for mat in range(4)] + [jax.ShapeDtypeStruct(m.shape, f32) for m in masters] * 3 + [jax.ShapeDtypeStruct((1,), f32)],
        in_specs=[hbm] * 3 + [vmem],
        out_specs=[hbm] * 16 + [smem],
        scratch_shapes=[
            pltpu.VMEM((4,) + split, bf16), pltpu.VMEM(up_shape, f32), pltpu.VMEM(down_shape, f32),
            dma((4, 4)), dma((2,)), dma((4, 4, 4)), dma((3, 4)),
        ],
        compiler_params=pltpu.CompilerParams(vmem_limit_bytes=50 * 1024 * 1024),
    )(outs[0].reshape((4,) + split), *outs[1:])
    weights = [placed[mat].reshape(masters[mat].shape[0] * 128, -1) for mat in range(4)]
    return tuple(weights) + tuple(placed[4:16]) + (placed[16][0],)


def mat_nt(left, right):
    return lax.dot_general(left, right, (((1,), (1,)), ((), ())), preferred_element_type=jnp.float32)


def mat_tn(left, right):
    return lax.dot_general(left, right, (((0,), (0,)), ((), ())), preferred_element_type=jnp.float32)


def gelu_pair(pre):
    normal_cdf = 0.5 * (1.0 + lax.erf(pre * ROOT_HALF))
    density = jnp.exp(-0.5 * pre * pre) * INV_ROOT_TAU
    return pre * normal_cdf, normal_cdf + pre * density


def fwd_bwd(rows_in, rows_grad, w_up1, w_down1, w_up2, w_down2):
    pre_up1 = jnp.dot(rows_in, w_up1, preferred_element_type=jnp.float32)
    gel_up1, der_up1 = gelu_pair(pre_up1)
    act_up1 = gel_up1.astype(jnp.bfloat16)
    mid_act = jnp.dot(act_up1, w_down1, preferred_element_type=jnp.float32).astype(jnp.bfloat16)
    pre_up2 = jnp.dot(mid_act, w_up2, preferred_element_type=jnp.float32)
    gel_up2, der_up2 = gelu_pair(pre_up2)
    act_up2 = gel_up2.astype(jnp.bfloat16)
    grad_act2 = mat_nt(rows_grad, w_down2).astype(jnp.bfloat16)
    grad_pre2 = (grad_act2.astype(jnp.float32) * der_up2).astype(jnp.bfloat16)
    grad_mid = mat_nt(grad_pre2, w_up2).astype(jnp.bfloat16)
    grad_act1 = mat_nt(grad_mid, w_down1).astype(jnp.bfloat16)
    grad_pre1 = (grad_act1.astype(jnp.float32) * der_up1).astype(jnp.bfloat16)
    return ((rows_in, grad_pre1), (act_up1, grad_mid), (mid_act, grad_pre2), (act_up2, rows_grad))


def solution(mesh):
    rows_spec = P("data", None)
    full_spec = P(None, None)
    scalar_spec = P()

    def shard_body(act_in, grad_out, w_up1, w_down1, w_up2, w_down2, *rest):
        pairs = fwd_bwd(act_in, grad_out, w_up1, w_down1, w_up2, w_down2)
        grads = [mat_tn(left, right) for left, right in pairs]
        return comm_call(768, grads, rest[0:4], rest[4:8], rest[8:12], rest[12], rest[13])

    in_specs = (rows_spec, rows_spec) + (full_spec,) * 4 + (rows_spec,) * 12 + (scalar_spec, scalar_spec)
    out_specs = (full_spec,) * 4 + (rows_spec,) * 12 + (scalar_spec,)
    return jax.shard_map(shard_body, mesh=mesh, in_specs=in_specs, out_specs=out_specs, check_vma=False)
```

profile of v0, /device:TPU:1, one launch (start us, length us, event | category | flops | bytes accessed | tf_op | source)
XLA Modules:
  0.0 267.8 jit_solution(5867180821163186196)
XLA Ops:
  1.9 0.0 copy-start.4
  2.0 0.0 slice-start
  2.0 10.8 %multiply_convert_fusion.1 = (bf16[1024,3072]{1,0:T(8,128)(2,1)S(1)}, f32[1024,3072]{1,0:T(8,128)}) fusion(bf16[1024,768]{1,0:T(8,128)(2,1)} %param.20, bf16[768,3072]{1,0:T(8,128)(2,1)} %param.22), kind=kOutput, calls=%fused_computation.16 | convolution fusion | flops 4847566848 | bytes 25165824 | tf_op jit(solution)/shard_map/dot_general | solution.py:462
  12.8 0.0 copy-start.9
  12.8 0.0 copy-done.4
  12.8 0.0 copy-start.3
  12.8 0.0 slice-start.1
  12.8 5.0 %convolution_convert_fusion.1 = bf16[1024,768]{1,0:T(8,128)(2,1)S(1)} fusion(bf16[1024,3072]{1,0:T(8,128)(2,1)S(1)} %get-tuple-element.59, bf16[3072,768]{1,0:T(8,128)(2,1)S(1)} %copy-done.4), kind=kOutput, calls=%fused_computation.25 | convolution fusion | flops 4832624640 | bytes 12582912 | tf_op jit(solution)/shard_map/dot_general | solution.py:465
  17.8 0.0 copy-done.9
  17.9 0.0 copy-done.3
  17.9 0.0 copy-start.5
  17.9 7.9 %fusion.22 = f32[1024,3072]{1,0:T(8,128)} fusion(bf16[1024,768]{1,0:T(8,128)(2,1)S(1)} %convolution_convert_fusion.1, bf16[768,3072]{1,0:T(8,128)(2,1)S(1)} %copy-done.3), kind=kOutput, calls=%fused_computation.28 | convolution fusion | flops 4831838208 | bytes 18874368 | tf_op jit(solution)/shard_map/dot_general | solution.py:466
  25.8 0.0 slice-done
  25.8 0.0 slice-done.1
  25.8 0.0 copy-done.5
  25.8 10.9 %fusion.5 = bf16[1024,3072]{1,0:T(8,128)(2,1)S(1)} fusion(f32[1024,3072]{1,0:T(8,128)} %fusion.22, bf16[1024,768]{1,0:T(8,128)(2,1)S(1)} %copy-done.5, bf16[3072,768]{1,0:T(8,128)(2,1)S(1)} %bitcast.40), kind=kOutput, calls=%fused_computation.7 | convolution fusion | flops 4869586944 | bytes 25165824 | tf_op jit(solution)/shard_map/dot_general | solution.py:448
  36.8 0.0 copy-start.7
  36.8 13.5 %fusion.12 = f32[3072,768]{1,0:T(8,128)} fusion(bf16[1024,768]{1,0:T(8,128)(2,1)S(1)} %copy-done.5, f32[1024,3072]{1,0:T(8,128)} %fusion.22), kind=kOutput, calls=%fused_computation.18 | convolution fusion | flops 4847566848 | bytes 23592960 | tf_op jit(solution)/shard_map/dot_general | solution.py:452
  50.3 0.0 copy-done.7
  50.3 0.0 copy-start.6
  50.3 6.2 %convolution_convert_fusion = bf16[1024,768]{1,0:T(8,128)(2,1)} fusion(bf16[1024,3072]{1,0:T(8,128)(2,1)S(1)} %fusion.5, bf16[768,3072]{1,0:T(8,128)(2,1)S(1)} %copy-done.3), kind=kOutput, calls=%fused_computation.24 | convolution fusion | flops 4832624640 | bytes 12582912 | tf_op jit(solution)/shard_map/dot_general | solution.py:448
  56.5 0.0 copy-done.6
  56.5 17.0 %fusion.13 = f32[3072,768]{0,1:T(8,128)} fusion(bf16[1024,768]{1,0:T(8,128)(2,1)S(1)} %copy-done.6, f32[1024,3072]{1,0:T(8,128)} %get-tuple-element.60, bf16[1024,768]{1,0:T(8,128)(2,1)} %convolution_convert_fusion, bf16[3072,768]{1,0:T(8,128)(2,1)} %param.23), kind=kOutput, calls=%fused_computation.19 | convolution fusion | flops 9701425152 | bytes 29884416 | tf_op jit(solution)/shard_map/dot_general | solution.py:452
  73.5 0.0 copy-start.8
  73.5 10.1 %fusion.23 = f32[3072,768]{1,0:T(8,128)} fusion(bf16[1024,3072]{1,0:T(8,128)(2,1)} %copy-done.9, bf16[1024,768]{1,0:T(8,128)(2,1)} %convolution_convert_fusion), kind=kOutput, calls=%fused_computation.29 | convolution fusion | flops 4831838208 | bytes 17301504 | tf_op jit(solution)/shard_map/dot_general | solution.py:452
  83.6 0.0 copy-done.8
  83.6 7.6 %fusion.24 = f32[768,3072]{1,0:T(8,128)} fusion(bf16[1024,768]{1,0:T(8,128)(2,1)S(1)} %convolution_convert_fusion.1, bf16[1024,3072]{1,0:T(8,128)(2,1)S(1)} %copy-done.8), kind=kOutput, calls=%fused_computation.30 | convolution fusion | flops 4831838208 | bytes 17301504 | tf_op jit(solution)/shard_map/dot_general | solution.py:452
  91.2 159.0 %reduce_update_gather.1 = (bf16[4,4,4,4,2,24,768]{6,5,4,3,2,1,0:T(8,128)(2,1)}, f32[3,2,6,3072]{3,2,1,0:T(8,128)}, f32[3,2,24,768]{3,2,1,0:T(8,128)}, f32[8,128]{1,0:T(8,128)}) custom-call(f32[4,4,2,24,3072]{4,3,2,1,0:T(8,128)} %bitcast.36, f32[4,4,4,2,24,768]{5,4,3,2,1,0:T(8,128)} %bitcast.37, f32[4,4,2,24,3072]{4,3,2,1,0:T(8,128)} %bitcast.38, ...), custom_call_target="tpu_custom_call" | custom-call | tf_op jit(solution)/shard_map/reduce_update_gather/pallas_call | solution.py:421
  250.2 0.0 copy-start
  250.3 1.1 copy-done
  251.3 0.0 copy-start.1
  251.3 1.0 copy-done.1
  252.3 0.0 copy-start.2
  252.3 0.7 copy-done.2
  253.0 14.6 %place_outputs.1 = (bf16[4,4,2,24,3072]{4,3,2,1,0:T(8,128)(2,1)}, bf16[4,4,2,2,2,24,768]{6,5,4,3,2,1,0:T(8,128)(2,1)}, bf16[4,4,2,24,3072]{4,3,2,1,0:T(8,128)(2,...) custom-call(bf16[4,4,4,2,2,2,24,768]{7,6,5,4,3,2,1,0:T(8,128)(2,1)} , ...), custom_call_target="tpu_custom_call" | custom-call | tf_op jit(solution)/shard_map/place_outputs/pallas_call | solution.py:431
  (1 shorter events, 0.0 us)
Async XLA Ops:
  1.9 10.8 %copy-start.4 = (bf16[3072,768]{1,0:T(8,128)(2,1)S(1)}, bf16[3072,768]{1,0:T(8,128)(2,1)}, u32[]{:S(2)}) copy-start(bf16[3072,768]{1,0:T(8,128)(2,1)} %param.23) | copy-start | bytes 14155780
  2.0 23.9 %slice-start = ((s8[4718592]{0:T(1024)(128)(4,1)}), s8[4194304]{0:T(1024)(128)(4,1)S(1)}, s32[]{:S(2)}) async-start(s8[4718592]{0:T(1024)(128)(4,1)} %bitcast.39), calls=%async_computation | async-start | bytes 8388608
  12.8 5.1 %copy-start.9 = (bf16[1024,3072]{1,0:T(8,128)(2,1)}, bf16[1024,3072]{1,0:T(8,128)(2,1)S(1)}, u32[]{:S(2)}) copy-start(bf16[1024,3072]{1,0:T(8,128)(2,1)S(1)} %get-tuple-element.59) | copy-start | bytes 18874372
  12.8 5.1 %copy-start.3 = (bf16[768,3072]{1,0:T(8,128)(2,1)S(1)}, bf16[768,3072]{1,0:T(8,128)(2,1)}, u32[]{:S(2)}) copy-start(bf16[768,3072]{1,0:T(8,128)(2,1)} %param.24) | copy-start | bytes 14155780
  12.8 13.0 %slice-start.1 = ((s8[4718592]{0:T(1024)(128)(4,1)}), s8[524288]{0:T(1024)(128)(4,1)S(1)}, s32[]{:S(2)}) async-start(s8[4718592]{0:T(1024)(128)(4,1)} %bitcast.39), calls=%async_computation.1 | async-start | bytes 1048576
  17.9 8.0 %copy-start.5 = (bf16[1024,768]{1,0:T(8,128)(2,1)S(1)}, bf16[1024,768]{1,0:T(8,128)(2,1)}, u32[]{:S(2)}) copy-start(bf16[1024,768]{1,0:T(8,128)(2,1)} %param.21) | copy-start | bytes 4718596
  36.8 13.5 %copy-start.7 = (bf16[1024,3072]{1,0:T(8,128)(2,1)}, bf16[1024,3072]{1,0:T(8,128)(2,1)S(1)}, u32[]{:S(2)}) copy-start(bf16[1024,3072]{1,0:T(8,128)(2,1)S(1)} %fusion.5) | copy-start | bytes 18874372
  50.3 6.2 %copy-start.6 = (bf16[1024,768]{1,0:T(8,128)(2,1)S(1)}, bf16[1024,768]{1,0:T(8,128)(2,1)}, u32[]{:S(2)}) copy-start(bf16[1024,768]{1,0:T(8,128)(2,1)} %param.20) | copy-start | bytes 4718596
  73.5 10.1 %copy-start.8 = (bf16[1024,3072]{1,0:T(8,128)(2,1)S(1)}, bf16[1024,3072]{1,0:T(8,128)(2,1)}, u32[]{:S(2)}) copy-start(bf16[1024,3072]{1,0:T(8,128)(2,1)} %copy-done.7) | copy-start | bytes 18874372
  250.2 1.1 copy-start
  251.3 1.0 copy-start.1
  252.3 0.7 copy-start.2
where the time goes:
time: 268 us
  Pallas kernels  174 us (65%)
  matrix products  89.1 us (33%)
  local copies, waits for them, and re-layouts  2.8 us (1%)
    pallas_call x1, Pallas kernels, comm_call(): pl.pallas_call(functools.partial(comm_kernel, lanes), name='reduce_update...  159 us
    dot_general x4, matrix products, mat_tn(): lax.dot_general(left, right, (((0,), (0,)), ((), ())), preferred_element_...  48.2 us
    dot_general x2, matrix products, mat_nt(): lax.dot_general(left, right, (((1,), (1,)), ((), ())), preferred_element_...  17.2 us
    pallas_call x1, Pallas kernels, comm_call(): pl.pallas_call(functools.partial(place_kernel, lanes), name='place_output...  14.6 us
    dot_general x1, matrix products, fwd_bwd(): pre_up1 = jnp.dot(rows_in, w_up1, preferred_element_type=jnp.float32)  10.8 us
    dot_general x1, matrix products, fwd_bwd(): pre_up2 = jnp.dot(mid_act, w_up2, preferred_element_type=jnp.float32)  7.94 us

commit v1 on v0

v1 whole, which is shorter than its diff:
```python
import functools
import math
import jax
import jax.numpy as jnp
from jax import lax
from jax.experimental import pallas as pl
from jax.experimental.pallas import tpu as pltpu
from jax.sharding import PartitionSpec as P

STEP = 20
BETA_ONE = 0.9
BETA_TWO = 0.95
EPSILON = 1e-8
NORM_EPS = 1e-6
CORR_ONE = 1.0 - BETA_ONE ** STEP
CORR_TWO = 1.0 - BETA_TWO ** STEP
ROOT_HALF = math.sqrt(0.5)
INV_ROOT_TAU = 1.0 / math.sqrt(2.0 * math.pi)

MESH = pl.DeviceIdType.MESH
STRIDES = (32, 8, 2)
ORDERS = ((2, 1, 0), (1, 0, 2), (0, 2, 1))
ROWS = 24
SUB = 6
CHUNK = 8
SIDE = 4
COLOURS = 3
SIDES = 2
ALL = slice(None)
TILE = 512


def adam_step(scaled, master_old, mom_old, vel_old, learn_rate):
    mom_new = BETA_ONE * mom_old + (1.0 - BETA_ONE) * scaled
    vel_new = BETA_TWO * vel_old + (1.0 - BETA_TWO) * scaled * scaled
    master_new = master_old - learn_rate * (mom_new / CORR_ONE) / (jnp.sqrt(vel_new / CORR_TWO) + EPSILON)
    return master_new, mom_new, vel_new


def comm_kernel(lanes, *refs):
    (g_down2, grad_rows, mid_rows, in_rows, w_down1, w_up2, w_down2, der1, der2, act1), refs = refs[:10], refs[10:]
    states, refs = refs[:12], refs[12:]
    (lr_ref, clip_ref), refs = refs[:2], refs[2:]
    (w_out, up_out, down_out, norm_out, g_up1, g_down1, g_up2), refs = refs[:7], refs[7:]
    (total, peer_in, rs1, rs2, rs3, norm_core, norm_axis, send_g, recv_g, send_w, recv_w, block_tmp, w_own, up_state, down_state), refs = refs[:15], refs[15:]
    (left, flipped, mid_acc, mid_grad, w_tile, act_tile, der_tile, out_tile), refs = refs[:8], refs[8:]
    (load_sem, state_sem, pair_s, pair_r, rs1_s, rs1_r, rs2_s, rs2_r, rs3_s, rs3_r, nc_s, nc_r, na_s, na_r, xg_s, xg_r, xw_s, xw_r, own_sem, ag_s, ag_r, out_s, out_r) = refs[:23]
    row_sem, tile_sem, store_sem, pair_credit, ring_credit = refs[23:]
    half = lanes // 2
    me = lax.axis_index("data")
    core = lax.rem(me, SIDES)
    member = lax.rem(me, 4)
    pos = (me // 32, lax.rem(me // 8, 4), lax.rem(me // 2, 4))
    partner = me + 1 - 2 * core

    def device(axis, coord):
        return me + (coord - pos[axis]) * STRIDES[axis]

    def step(axis, hops):
        return lax.rem(pos[axis] + hops, 4)

    def remote(src, dst, send_sem, recv_sem, target):
        return pltpu.make_async_remote_copy(src_ref=src, dst_ref=dst, send_sem=send_sem, recv_sem=recv_sem, device_id=(target,), device_id_type=MESH)

    peers = [partner] + [device(axis, step(axis, hops)) for axis in range(COLOURS) for hops in (1, 2, 3)]
    peers.append(me - member + lax.rem(member + 2, 4) + 1 - 2 * core)
    barrier = pltpu.get_barrier_semaphore()
    for peer in peers:
        pl.semaphore_signal(barrier, device_id=(peer,), device_id_type=MESH)

    grads = (g_up1, g_down1, g_up2, g_down2)
    mat_order = (3, 2, 1, 0)
    pair_slot = (1, 0, 1, 0)
    loads, pairs = {0: [], 2: []}, {0: [], 2: []}

    def issue_up(mat, x_low):
        for x in (x_low, x_low + 2):
            for owner in (1 - core, core):
                col = pl.multiple_of((x_low * 2 + owner) * lanes, lanes)
                src = grads[mat].at[:, :, x // SIDES, :, pl.ds(col, lanes)]
                if owner is core:
                    loads[mat].append(pltpu.make_async_copy(src, total.at[mat, :, :, x], load_sem.at[mat, x]))
                    loads[mat][-1].start()
                else:
                    pairs[mat].append(remote(src, peer_in.at[pair_slot[mat], :, :, x], pair_s.at[mat, x], pair_r.at[mat, x], partner))
                    pairs[mat][-1].start()

    def issue_rows(low, high):
        def move(i, carry):
            place = (i // 16, lax.rem(i // SIDE, 4), lax.rem(i, SIDE))
            there = g_down1.at[pl.ds(pl.multiple_of(i * 2 * ROWS + (1 - core) * ROWS, 8), ROWS)]
            here = g_down1.at[pl.ds(pl.multiple_of(i * 2 * ROWS + core * ROWS, 8), ROWS)]
            remote(there, peer_in.at[(pair_slot[1],) + place], pair_s.at[1, 0], pair_r.at[1, 0], partner).start()
            pltpu.make_async_copy(here, total.at[(1,) + place], load_sem.at[1, 0]).start()
            return carry

        lax.fori_loop(low, high, move, 0)

    loads[1] = [pltpu.make_async_copy(total.at[1], total.at[1], load_sem.at[1, 0])]
    pairs[1] = [remote(peer_in.at[pair_slot[1]], peer_in.at[pair_slot[1]], pair_s.at[1, 0], pair_r.at[1, 0], partner)]
    loads[3] = [pltpu.make_async_copy(g_down2.at[:, :, :, core], total.at[3], load_sem.at[3, 0])]
    loads[3][0].start()

    tiles = SIDE * lanes // TILE

    def span(t):
        return pl.ds(pl.multiple_of(t * TILE, TILE), TILE)

    def fetch_a(t, slot):
        return [
            pltpu.make_async_copy(w_down2.at[span(t)], w_tile.at[slot], tile_sem.at[slot, 0]),
            pltpu.make_async_copy(w_up2.at[:, span(t)], act_tile.at[slot, pl.ds(0, lanes)], tile_sem.at[slot, 1]),
            pltpu.make_async_copy(der2.at[:, span(t)], der_tile.at[slot], tile_sem.at[slot, 2]),
        ]

    def fetch_b(t, slot):
        return [
            pltpu.make_async_copy(w_down1.at[span(t)], w_tile.at[slot], tile_sem.at[slot, 0]),
            pltpu.make_async_copy(act1.at[:, span(t)], act_tile.at[slot], tile_sem.at[slot, 1]),
            pltpu.make_async_copy(der1.at[:, span(t)], der_tile.at[slot], tile_sem.at[slot, 2]),
        ]

    def begin(copies):
        for copy in copies:
            copy.start()

    def end(copies):
        for copy in copies:
            copy.wait()

    row_loads = [pltpu.make_async_copy(grad_rows, left, row_sem.at[0]), pltpu.make_async_copy(mid_rows, mid_grad, row_sem.at[1])]
    begin(row_loads)
    begin(fetch_a(0, 0))
    state_loads = []
    for field in range(COLOURS):
        for mat in range(SIDE):
            dst = (down_state if mat % SIDES else up_state).at[field, mat // SIDES]
            state_loads.append(pltpu.make_async_copy(states[4 * field + mat], dst, state_sem.at[field, mat]))
    begin(state_loads)
    def store_a(t, slot):
        return [pltpu.make_async_copy(out_tile.at[slot], g_up2.at[:, :, :, :, span(t)], store_sem.at[slot, 0])]

    def store_b(t, slot):
        return [
            pltpu.make_async_copy(out_tile.at[slot], g_up1.at[:, :, :, :, span(t)], store_sem.at[slot, 0]),
            pltpu.make_async_copy(mid_acc.at[slot], g_down1.at[span(t)], store_sem.at[slot, 1]),
        ]

    def run(first, last, fetch, store, work):
        def tile(t, carry):
            slot = lax.rem(t, SIDES)

            @pl.when(t + 1 < tiles)
            def _():
                begin(fetch(t + 1, 1 - slot))

            end(fetch(t, slot))

            @pl.when(t - first >= 2)
            def _():
                end(store(t - 2, slot))

            work(slot)
            begin(store(t, slot))
            return carry

        lax.fori_loop(first, last, tile, 0)
        for t in range(max(first, last - 2), last):
            end(store(t, t % 2))

    def dot(lhs, rhs, lhs_dim, rhs_dim):
        return lax.dot_general(lhs, rhs, (((lhs_dim,), (rhs_dim,)), ((), ())), preferred_element_type=jnp.float32)

    def work_a(slot):
        grad_act2 = dot(left[...], w_tile[slot], 1, 1).astype(jnp.bfloat16)
        grad_pre2 = (grad_act2.astype(jnp.float32) * der_tile[slot]).astype(jnp.bfloat16)
        out_tile[slot] = dot(flipped[...], grad_pre2, 1, 0).reshape(out_tile.shape[1:])
        mid_acc[...] += dot(grad_pre2, act_tile[slot, pl.ds(0, lanes)], 1, 1).reshape(mid_acc.shape)

    def work_b(slot):
        mid_acc[slot] = dot(act_tile[slot], mid_grad[...], 0, 0)
        grad_act1 = dot(mid_grad[...], w_tile[slot], 1, 1).astype(jnp.bfloat16)
        grad_pre1 = (grad_act1.astype(jnp.float32) * der_tile[slot]).astype(jnp.bfloat16)
        out_tile[slot] = dot(flipped[...], grad_pre1, 1, 0).reshape(out_tile.shape[1:])

    end(row_loads)
    flipped[...] = mid_grad[...].T
    mid_acc[...] = jnp.zeros_like(mid_acc)
    run(0, 1, fetch_a, store_a, work_a)
    pl.semaphore_wait(barrier, len(peers))
    pairs[3] = [remote(g_down2.at[:, :, :, 1 - core], peer_in.at[pair_slot[3]], pair_s.at[3, 0], pair_r.at[3, 0], partner)]
    pairs[3][0].start()

    def part(mats, coords, colour, side):
        index = [mats, ALL, ALL, ALL, pl.ds(CHUNK * colour, CHUNK), pl.ds(half * side, half)]
        for axis, coord in coords.items():
            index[1 + axis] = coord
        return tuple(index)

    class Phase:
        def __init__(self, level, base, buf, send_sem, recv_sem):
            self.level, self.base, self.buf, self.send_sem, self.recv_sem = level, base, buf, send_sem, recv_sem
            self.mats, self.count = (slice(base, base + 2), 2) if level else (base, 4)
            self.copies = {}

        def where(self, colour, coord):
            order = ORDERS[colour]
            coords = {axis: pos[axis] for axis in order[:self.level]}
            coords[order[self.level]] = coord
            return coords

        def row(self, colour, coord, side, i):
            coords = self.where(colour, coord)
            if self.level:
                return part(self.base + i, coords, colour, side)
            coords[min(axis for axis in range(COLOURS) if axis not in coords)] = i
            return part(self.mats, coords, colour, side)

        def send(self, colour, side, kind, src, target):
            copy = remote(src, self.buf.at[colour, side, kind], self.send_sem.at[colour, side, kind], self.recv_sem.at[colour, side, kind], target)
            copy.start()
            self.copies[colour, side, kind] = copy

        def near(self, colour, side):
            axis = ORDERS[colour][self.level]
            coord = step(axis, 1 if side == 0 else 3)
            return coord, device(axis, coord)

        def start(self):
            for kind in range(SIDES):
                for colour in range(COLOURS):
                    for side in range(SIDES):
                        coord, target = self.near(colour, side)
                        aim = step(ORDERS[colour][self.level], 2) if kind == 0 else coord
                        src = total.at[part(self.mats, self.where(colour, aim), colour, side if kind == 0 else 1 - side)]
                        self.send(colour, side, kind, src, target)

        def forward(self):
            for colour in range(COLOURS):
                for side in range(SIDES):
                    coord, target = self.near(colour, side)
                    self.copies[colour, side, 0].wait_recv()

                    def add_own(i, carry, colour=colour, side=side, coord=coord):
                        self.buf[colour, side, 0, i] = self.buf[colour, side, 0, i] + total[self.row(colour, coord, side, i)]
                        return carry

                    lax.fori_loop(0, self.count, add_own, 0)
                    self.send(colour, side, 2, self.buf.at[colour, side, 0], target)

        def finish(self):
            for colour in range(COLOURS):
                for side in range(SIDES):
                    self.copies[colour, 1 - side, 1].wait_recv()
                    self.copies[colour, side, 2].wait_recv()

                    def add_both(i, carry, colour=colour, side=side):
                        own = self.row(colour, pos[ORDERS[colour][self.level]], side, i)
                        total[own] = total[own] + (self.buf[colour, 1 - side, 1, i] + self.buf[colour, side, 2, i])
                        return carry

                    lax.fori_loop(0, self.count, add_both, 0)

        def drain(self):
            for copy in self.copies.values():
                copy.wait_send()

    ring_slot = (1, 0, 1, 0)
    first = {mat: Phase(0, mat, rs1.at[ring_slot[mat]], rs1_s.at[mat], rs1_r.at[mat]) for mat in mat_order}

    def add_pair(mat):
        end(loads[mat])
        for copy in pairs[mat]:
            copy.wait_recv()

        def add(i, carry):
            total[mat, i // SIDE, lax.rem(i, SIDE)] = total[mat, i // SIDE, lax.rem(i, SIDE)] + peer_in[pair_slot[mat], i // SIDE, lax.rem(i, SIDE)]
            return carry

        lax.fori_loop(0, 16, add, 0)
        if mat >= 2:
            pl.semaphore_signal(pair_credit, device_id=(partner,), device_id_type=MESH)

    ring = [device(axis, step(axis, hops)) for axis in range(COLOURS) for hops in (1, 3)]

    def close(mat):
        first[mat].finish()
        first[mat].drain()
        for peer in ring:
            pl.semaphore_signal(ring_credit.at[ring_slot[mat]], device_id=(peer,), device_id_type=MESH)

    second = {base: Phase(1, base, rs2.at[base // 2], rs2_s.at[base // 2], rs2_r.at[base // 2]) for base in (2, 0)}
    third = {base: Phase(2, base, rs3.at[base // 2], rs3_s.at[base // 2], rs3_r.at[base // 2]) for base in (2, 0)}
    run(1, 4, fetch_a, store_a, work_a)
    add_pair(3)
    first[3].start()
    issue_up(2, 0)
    run(4, tiles, fetch_a, store_a, work_a)
    issue_up(2, 1)
    begin(fetch_b(0, 0))
    in_load = pltpu.make_async_copy(in_rows, left, row_sem.at[0])
    in_load.start()
    first[3].forward()
    mid_grad[...] = mid_acc[...].reshape(mid_grad.shape).astype(jnp.bfloat16)
    in_load.wait()
    flipped[...] = left[...].T
    run(0, 2, fetch_b, store_b, work_b)
    add_pair(2)
    first[2].start()
    run(2, 4, fetch_b, store_b, work_b)
    first[2].forward()
    pl.semaphore_wait(pair_credit, 1)
    issue_rows(0, 32)
    pl.semaphore_wait(pair_credit, 1)
    issue_up(0, 0)
    close(3)
    run(4, tiles, fetch_b, store_b, work_b)
    issue_rows(32, 64)
    issue_up(0, 1)
    close(2)
    second[2].start()
    add_pair(1)
    pl.semaphore_wait(ring_credit.at[0], len(ring))
    first[1].start()
    second[2].forward()
    add_pair(0)
    pl.semaphore_wait(ring_credit.at[1], len(ring))
    first[0].start()
    second[2].finish()
    third[2].start()
    first[1].forward()
    third[2].forward()
    first[1].finish()
    third[2].finish()
    first[0].forward()
    first[0].finish()
    second[0].start()
    second[0].forward()
    second[0].finish()
    third[0].start()
    third[0].forward()
    third[0].finish()

    group_scale = 1.0 / 128.0
    grad_own = [total[mat, pos[0], pos[1], pos[2]] * group_scale for mat in range(SIDE)]
    partial = None
    for block in grad_own:
        square = block * block
        for row in range(ROWS // 8):
            for col in range(max(1, lanes // 128)):
                tile = square[8 * row:8 * row + 8, 128 * col:128 * col + 128]
                partial = tile if partial is None else partial + tile
    norm_core[core] = partial
    swap = remote(norm_core.at[core], norm_core.at[core], nc_s.at[0], nc_r.at[0], partner)
    swap.start()
    for target in range(SIDE):
        for i, mat in enumerate((0, 2)):
            send_g[target, i] = grad_own[mat][SUB * target:SUB * target + SUB]
    moves = []
    for hops in range(1, SIDE):
        other = lax.rem(member + hops, SIDE)
        copy = remote(send_g.at[other], recv_g.at[member], xg_s.at[hops - 1], xg_r.at[hops - 1], me - member + other)
        copy.start()
        moves.append(copy)
    recv_g[member] = send_g[member]
    swap.wait_recv()
    running = norm_core[0] + norm_core[1]
    sends = [swap] + moves
    for axis in (2, 1, 0):
        norm_axis[axis, pos[axis]] = running
        copies = []
        for hops in (1, 2, 3):
            coord = step(axis, hops)
            copy = remote(norm_axis.at[axis, pos[axis]], norm_axis.at[axis, pos[axis]], na_s.at[axis, hops - 1], na_r.at[axis, hops - 1], device(axis, coord))
            copy.start()
            copies.append(copy)
        for copy in copies:
            copy.wait_recv()
        sends = sends + copies
        running = (norm_axis[axis, 0] + norm_axis[axis, 1]) + (norm_axis[axis, 2] + norm_axis[axis, 3])
    norm = jnp.sqrt(jnp.sum(jnp.sum(running, axis=1, keepdims=True), axis=0, keepdims=True))
    norm_out[...] = jnp.broadcast_to(norm, norm_out.shape)
    clip_scale = jnp.minimum(1.0, clip_ref[0] / (norm + NORM_EPS))
    learn_rate = lr_ref[0]

    end(state_loads)
    for i in range(SIDES):
        fresh = adam_step(grad_own[2 * i + 1] * clip_scale, down_state[0, i], down_state[1, i], down_state[2, i], learn_rate)
        for field in range(COLOURS):
            down_state[field, i] = fresh[field]
        w_own[2 + i] = fresh[0].astype(jnp.bfloat16)

    def spot(group, coords, colour, side):
        lane = ALL if side is None else pl.ds(half * side, half)
        index = [pl.ds(2 * group, 2), ALL, ALL, ALL, core, pl.ds(CHUNK * colour, CHUNK), lane]
        for axis, coord in coords.items():
            index[1 + axis] = coord
        return w_out.at[tuple(index)]

    handed = []

    class Gather:
        def __init__(self, group, level):
            self.group, self.level = group, level
            self.copies = {}

        def spot(self, colour, coord, side):
            order = ORDERS[colour]
            coords = {axis: pos[axis] for axis in order[:self.level]}
            coords[order[self.level]] = coord
            return spot(self.group, coords, colour, side)

        def near(self, colour, side):
            axis = ORDERS[colour][self.level]
            coord = step(axis, 1 if side == 0 else 3)
            return coord, device(axis, coord)

        def send(self, colour, side, kind, src, dst):
            spots = (self.group, self.level, colour, side, kind)
            copy = remote(src, dst, ag_s.at[spots], ag_r.at[spots], self.near(colour, side)[1])
            copy.start()
            self.copies[colour, side, kind] = copy

        def hand(self, ref, slot):
            copy = remote(ref, ref, out_s.at[self.group, slot], out_r.at[self.group, slot], partner)
            copy.start()
            handed.append(copy)

        def start(self):
            for kind in range(SIDES):
                for colour in range(COLOURS):
                    for side in range(SIDES):
                        lane_side = side if kind == 0 else 1 - side
                        dst = self.spot(colour, pos[ORDERS[colour][self.level]], lane_side)
                        src = dst
                        if self.level == 2:
                            src = w_own.at[pl.ds(2 * self.group, 2), pl.ds(CHUNK * colour, CHUNK), pl.ds(half * lane_side, half)]
                        self.send(colour, side, kind, src, dst)
            if self.level == 0:
                for colour in range(COLOURS):
                    self.hand(self.spot(colour, pos[ORDERS[colour][0]], None), 5 * colour)

        def forward(self):
            for colour in range(COLOURS):
                for side in range(SIDES):
                    self.copies[colour, side, 0].wait_recv()
                    ref = self.spot(colour, self.near(colour, 1 - side)[0], side)
                    self.send(colour, side, 2, ref, ref)

        def finish(self):
            for colour in range(COLOURS):
                for side in range(SIDES):
                    self.copies[colour, side, 1].wait_recv()
                    if self.level == 0:
                        self.hand(self.spot(colour, self.near(colour, 1 - side)[0], None), 5 * colour + 1 + side)
            for colour in range(COLOURS):
                for side in range(SIDES):
                    self.copies[colour, side, 2].wait_recv()
                    if self.level == 0:
                        self.hand(self.spot(colour, step(ORDERS[colour][0], 2), side), 5 * colour + 3 + side)

    keeps = [pltpu.make_async_copy(w_own.at[pl.ds(2 * group, 2)], w_out.at[pl.ds(2 * group, 2), pos[0], pos[1], pos[2], core], own_sem.at[group]) for group in range(SIDES)]
    gathers = {(group, level): Gather(group, level) for group in range(SIDES) for level in range(COLOURS)}
    gathers[1, 2].start()
    keeps[1].start()

    for copy in moves:
        copy.wait_recv()
    for i in range(SIDES):
        for col in range(SIDE):
            cols = slice(col * lanes, (col + 1) * lanes)
            scaled = recv_g[col, i] * clip_scale
            fresh = adam_step(scaled, up_state[0, i, :, cols], up_state[1, i, :, cols], up_state[2, i, :, cols], learn_rate)
            for field in range(COLOURS):
                up_state[field, i, :, cols] = fresh[field]
            send_w[col, i] = fresh[0]
    moves = []
    for hops in range(1, SIDE):
        other = lax.rem(member + hops, SIDE)
        copy = remote(send_w.at[other], recv_w.at[member], xw_s.at[hops - 1], xw_r.at[hops - 1], me - member + other)
        copy.start()
        moves.append(copy)
    recv_w[member] = send_w[member]
    state_stores = [pltpu.make_async_copy(up_state, up_out, state_sem.at[0, 0]), pltpu.make_async_copy(down_state, down_out, state_sem.at[0, 1])]
    begin(state_stores)
    gathers[1, 2].forward()
    for copy in moves:
        copy.wait_recv()
    sends = sends + moves
    for i in range(SIDES):
        for source in range(SIDE):
            block_tmp[SUB * source:SUB * source + SUB] = recv_w[source, i]
        w_own[i] = block_tmp[...].astype(jnp.bfloat16)
    gathers[0, 2].start()
    keeps[0].start()
    gathers[1, 2].finish()
    keeps[1].wait()
    gathers[1, 1].start()
    gathers[0, 2].forward()
    gathers[1, 1].forward()
    gathers[0, 2].finish()
    keeps[0].wait()
    gathers[0, 1].start()
    gathers[1, 1].finish()
    gathers[1, 0].start()
    gathers[0, 1].forward()
    gathers[0, 1].finish()
    gathers[0, 0].start()
    gathers[1, 0].forward()
    gathers[0, 0].forward()
    gathers[1, 0].finish()
    gathers[0, 0].finish()
    for gather in gathers.values():
        sends = sends + list(gather.copies.values())
    for phase in [first[1], first[0]] + list(second.values()) + list(third.values()):
        phase.drain()
    for mat in mat_order:
        for copy in pairs[mat]:
            copy.wait_send()
    for copy in sends:
        copy.wait_send()
    for copy in handed + state_stores:
        copy.wait()


def place_kernel(lanes, w_ref, up_ref, down_ref, norm_ref, *refs):
    weights, states, norm_out, (w_tmp, up_tmp, down_tmp, in_sem, state_in, out_sem, state_out) = refs[:4], refs[4:16], refs[16], refs[17:]
    norm_out[0] = jnp.max(norm_ref[...])
    loads = [[pltpu.make_async_copy(w_ref.at[mat % SIDES * 2 + mat // SIDES, z], w_tmp.at[mat, z], in_sem.at[mat, z]) for z in range(SIDE)] for mat in range(SIDE)]
    for row in loads:
        for copy in row:
            copy.start()
    state_loads = [pltpu.make_async_copy(up_ref, up_tmp, state_in.at[0]), pltpu.make_async_copy(down_ref, down_tmp, state_in.at[1])]
    for copy in state_loads:
        copy.start()
    stores = []
    for mat in range(SIDE):
        for z in range(SIDE):
            loads[mat][z].wait()
            if mat % SIDES:
                copies = [pltpu.make_async_copy(w_tmp.at[mat, z], weights[mat].at[z], out_sem.at[mat, z, 0])]
            else:
                copies = []
                for member in range(SIDE):
                    src = w_tmp.at[mat, z, :, :, member // SIDES, member % SIDES]
                    copies.append(pltpu.make_async_copy(src, weights[mat].at[z, :, :, :, pl.ds(member * lanes, lanes)], out_sem.at[mat, z, member]))
            for copy in copies:
                copy.start()
            stores = stores + copies
    for copy in state_loads:
        copy.wait()
    for field in range(COLOURS):
        for mat in range(SIDE):
            src = (down_tmp if mat % SIDES else up_tmp).at[field, mat // SIDES]
            copy = pltpu.make_async_copy(src, states[4 * field + mat], state_out.at[field, mat])
            copy.start()
            stores.append(copy)
    for copy in stores:
        copy.wait()


def comm_call(lanes, grad_down2, rows, weights_in, hidden, masters, moms, vels, learn_rate, clip_norm):
    up = (SIDE, SIDE, SIDES, ROWS, SIDE * lanes)
    down = (SIDE, SIDE, SIDE, SIDES, ROWS, lanes)
    local_rows = rows[0].shape[0]
    half = lanes // 2
    f32 = jnp.float32
    bf16 = jnp.bfloat16
    up_shape = (COLOURS, SIDES, SUB, SIDE * lanes)
    down_shape = (COLOURS, SIDES, ROWS, lanes)
    dma = pltpu.SemaphoreType.DMA
    vmem = pl.BlockSpec(memory_space=pltpu.VMEM)
    smem = pl.BlockSpec(memory_space=pltpu.SMEM)
    hbm = pl.BlockSpec(memory_space=pl.ANY)
    scratch = [
        pltpu.VMEM((SIDE, SIDE, SIDE, SIDE, ROWS, lanes), f32),
        pltpu.VMEM((SIDES, SIDE, SIDE, SIDE, ROWS, lanes), f32),
        pltpu.VMEM((SIDES, COLOURS, SIDES, COLOURS, SIDE, SIDE, CHUNK, half), f32),
        pltpu.VMEM((SIDES, COLOURS, SIDES, COLOURS, SIDES, SIDE, CHUNK, half), f32),
        pltpu.VMEM((SIDES, COLOURS, SIDES, COLOURS, SIDES, CHUNK, half), f32),
        pltpu.VMEM((2, 8, min(lanes, 128)), f32),
        pltpu.VMEM((3, 4, 8, min(lanes, 128)), f32),
        pltpu.VMEM((SIDE, SIDES, SUB, lanes), f32),
        pltpu.VMEM((SIDE, SIDES, SUB, lanes), f32),
        pltpu.VMEM((SIDE, SIDES, SUB, lanes), f32),
        pltpu.VMEM((SIDE, SIDES, SUB, lanes), f32),
        pltpu.VMEM((ROWS, lanes), f32),
        pltpu.VMEM((SIDE, ROWS, lanes), jnp.bfloat16),
        pltpu.VMEM(up_shape, f32),
        pltpu.VMEM(down_shape, f32),
        pltpu.VMEM((local_rows, lanes), bf16),
        pltpu.VMEM((lanes, local_rows), bf16),
        pltpu.VMEM((SIDES, local_rows // SIDES, lanes), f32),
        pltpu.VMEM((local_rows, lanes), bf16),
        pltpu.VMEM((SIDES, TILE, lanes), bf16),
        pltpu.VMEM((SIDES, local_rows, TILE), bf16),
        pltpu.VMEM((SIDES, local_rows, TILE), f32),
        pltpu.VMEM((SIDES, SIDE, SIDE, SIDES, ROWS, TILE), f32),
        dma((SIDE, SIDE)), dma((COLOURS, SIDE)), dma((SIDE, SIDE)), dma((SIDE, SIDE)),
        dma((SIDE, COLOURS, SIDES, COLOURS)), dma((SIDE, COLOURS, SIDES, COLOURS)), dma((SIDES, COLOURS, SIDES, COLOURS)), dma((SIDES, COLOURS, SIDES, COLOURS)), dma((SIDES, COLOURS, SIDES, COLOURS)), dma((SIDES, COLOURS, SIDES, COLOURS)),
        dma((1,)), dma((1,)), dma((COLOURS, COLOURS)), dma((COLOURS, COLOURS)), dma((COLOURS,)), dma((COLOURS,)), dma((COLOURS,)), dma((COLOURS,)),
        dma((SIDES,)), dma((SIDES, COLOURS, COLOURS, SIDES, COLOURS)), dma((SIDES, COLOURS, COLOURS, SIDES, COLOURS)), dma((SIDES, 15)), dma((SIDES, 15)),
        dma((SIDES,)), dma((SIDES, COLOURS)), dma((SIDES, SIDES)), pltpu.SemaphoreType.REGULAR, pltpu.SemaphoreType.REGULAR((2,)),
    ]
    outs = pl.pallas_call(
        functools.partial(comm_kernel, lanes),
        name="reduce_update_gather",
        out_shape=[jax.ShapeDtypeStruct((SIDE, SIDE, SIDE, SIDE, SIDES, ROWS, lanes), bf16), jax.ShapeDtypeStruct(up_shape, f32), jax.ShapeDtypeStruct(down_shape, f32), jax.ShapeDtypeStruct((8, 128), f32), jax.ShapeDtypeStruct(up, f32), jax.ShapeDtypeStruct((3072, lanes), f32), jax.ShapeDtypeStruct(up, f32)],
        in_specs=[hbm] * 22 + [smem] * 2,
        out_specs=[hbm] * 3 + [vmem] + [hbm] * 3,
        scratch_shapes=scratch,
        compiler_params=pltpu.CompilerParams(collective_id=0, has_side_effects=True, vmem_limit_bytes=67043328),
    )(grad_down2.reshape(down), *rows, *weights_in, *hidden, *masters, *moms, *vels, learn_rate.reshape(1), clip_norm.reshape(1))
    split = (SIDE, SIDE, SIDES, SIDES, SIDES, ROWS, lanes)
    placed = pl.pallas_call(
        functools.partial(place_kernel, lanes),
        name="place_outputs",
        out_shape=[jax.ShapeDtypeStruct(split if mat % SIDES else up, bf16) for mat in range(SIDE)] + [jax.ShapeDtypeStruct(m.shape, f32) for m in masters] * 3 + [jax.ShapeDtypeStruct((1,), f32)],
        in_specs=[hbm] * 3 + [vmem],
        out_specs=[hbm] * 16 + [smem],
        scratch_shapes=[
            pltpu.VMEM((SIDE,) + split, bf16), pltpu.VMEM(up_shape, f32), pltpu.VMEM(down_shape, f32),
            dma((SIDE, SIDE)), dma((SIDES,)), dma((SIDE, SIDE, SIDE)), dma((COLOURS, SIDE)),
        ],
        compiler_params=pltpu.CompilerParams(vmem_limit_bytes=67043328),
    )(outs[0].reshape((4,) + split), *outs[1:4])
    weights = [placed[mat].reshape(masters[mat].shape[0] * 128, -1) for mat in range(SIDE)]
    return tuple(weights) + tuple(placed[4:16]) + (placed[16][0],)


def mat_tn(left, right):
    return lax.dot_general(left, right, (((0,), (0,)), ((), ())), preferred_element_type=jnp.float32)


def gelu_pair(pre):
    normal_cdf = 0.5 * (1.0 + lax.erf(pre * ROOT_HALF))
    density = jnp.exp(-0.5 * pre * pre) * INV_ROOT_TAU
    return pre * normal_cdf, normal_cdf + pre * density


def solution(mesh):
    rows_spec = P("data", None)
    full_spec = P(None, None)
    scalar_spec = P()

    def shard_body(act_in, grad_out, w_up1, w_down1, w_up2, w_down2, *rest):
        gel_up1, der_up1 = gelu_pair(jnp.dot(act_in, w_up1, preferred_element_type=jnp.float32))
        act_up1 = gel_up1.astype(jnp.bfloat16)
        mid_act = jnp.dot(act_up1, w_down1, preferred_element_type=jnp.float32).astype(jnp.bfloat16)
        gel_up2, der_up2 = gelu_pair(jnp.dot(mid_act, w_up2, preferred_element_type=jnp.float32))
        grad_down2 = mat_tn(gel_up2.astype(jnp.bfloat16), grad_out)
        return comm_call(768, grad_down2, (grad_out, mid_act, act_in), (w_down1, w_up2, w_down2), (der_up1, der_up2, act_up1), rest[0:4], rest[4:8], rest[8:12], rest[12], rest[13])

    in_specs = (rows_spec, rows_spec) + (full_spec,) * 4 + (rows_spec,) * 12 + (scalar_spec, scalar_spec)
    out_specs = (full_spec,) * 4 + (rows_spec,) * 12 + (scalar_spec,)
    return jax.shard_map(shard_body, mesh=mesh, in_specs=in_specs, out_specs=out_specs, check_vma=False)
```

time: 268 us -> 234 us (0.87)
  matrix products: 89.1 us -> 35.7 us
  Pallas kernels: 174 us -> 193 us
    dot_general x4 -> x1, matrix products: 48.2 us -> 8.14 us  [mat_tn(): lax.dot_general(left, right, (((0,), (0,)), ((), ())), preferred_element_...]
    pallas_call x1, Pallas kernels: 159 us -> 178 us  [comm_call(): pl.pallas_call(functools.partial(comm_kernel, lanes), name='reduce_update...]
    dot_general x5 -> x3, matrix products: 40.9 us -> 27.5 us  [the longest x1 12 us: shard_body(): jnp.dot(act_in, w_up1, preferred_element_type=jnp.float32)]
where the time goes in v1:
time: 234 us
  Pallas kernels  193 us (82%)
  matrix products  35.7 us (15%)
  local copies, waits for them, and re-layouts  2.67 us (1%)
    pallas_call x1, Pallas kernels, comm_call(): pl.pallas_call(functools.partial(comm_kernel, lanes), name='reduce_update...  178 us
    pallas_call x1, Pallas kernels, comm_call(): pl.pallas_call(functools.partial(place_kernel, lanes), name='place_output...  15.5 us
    dot_general x1, matrix products, shard_body(): jnp.dot(act_in, w_up1, preferred_element_type=jnp.float32)  12 us
    dot_general x1, matrix products, shard_body(): jnp.dot(mid_act, w_up2, preferred_element_type=jnp.float32)  10.5 us
    dot_general x1, matrix products, mat_tn(): lax.dot_general(left, right, (((0,), (0,)), ((), ())), preferred_element_...  8.14 us
    dot_general x1, matrix products, shard_body(): jnp.dot(act_up1, w_down1, preferred_element_type=jnp.float32)  5.02 us

profile of v1, /device:TPU:1, one launch (start us, length us, event | category | flops | bytes accessed | tf_op | source)
XLA Modules:
  0.0 234.0 jit_solution(17894893814576139552)
XLA Ops:
  1.9 0.0 copy-start.1
  2.0 12.0 %fusion.3 = (f32[1024,3072]{1,0:T(8,128)}, bf16[1024,3072]{1,0:T(8,128)(2,1)S(1)}) fusion(bf16[1024,768]{1,0:T(8,128)(2,1)} %refs_3_.1, bf16[768,3072]{1,0:T(8,128)(2,1)} %param.22), kind=kOutput, calls=%fused_computation.5 | convolution fusion | flops 4863295488 | bytes 25165824 | tf_op jit(solution)/shard_map/dot_general | solution.py:647
  14.0 0.0 copy-start
  14.0 2.6 %copy-done = bf16[1024,3072]{1,0:T(8,128)(2,1)} copy-done((bf16[1024,3072]{1,0:T(8,128)(2,1)}, bf16[1024,3072]{1,0:T(8,128)(2,1)S(1)}, u32[]{:S(2)}) %copy-start) | copy-done | bytes 6291480
  16.7 0.0 copy-done.1
  16.7 0.0 copy-start.2
  16.7 5.0 %fusion.11.refs_2_ = bf16[1024,768]{1,0:T(8,128)(2,1)S(1)} fusion(bf16[1024,3072]{1,0:T(8,128)(2,1)S(1)} %get-tuple-element.60.refs_9_, bf16[3072,768]{1,0:T(8,128)(2,1)S(1)} %copy-done.1), kind=kOutput, calls=%fused_computation.17 | convolution fusion | flops 4831838208 | bytes 12582912 | tf_op jit(solution)/shard_map/dot_general | solution.py:649
  21.7 0.0 copy-done.2
  21.7 0.0 copy-start.4
  21.7 0.0 copy-start.3
  21.7 10.5 %fusion.7 = (f32[1024,3072]{1,0:T(8,128)}, f32[1024,3072]{1,0:T(8,128)S(1)}) fusion(bf16[1024,768]{1,0:T(8,128)(2,1)S(1)} %fusion.11.refs_2_, bf16[768,3072]{1,0:T(8,128)(2,1)S(1)} %copy-done.2), kind=kOutput, calls=%fused_computation.9 | convolution fusion | flops 4857004032 | bytes 31457280 | tf_op jit(solution)/shard_map/dot_general | solution.py:650
  32.2 0.0 copy-done.4
  32.2 0.0 copy-done.3
  32.2 8.1 %fusion.8 = f32[3072,768]{1,0:T(8,128)} fusion(bf16[1024,768]{1,0:T(8,128)(2,1)S(1)} %copy-done.3, f32[1024,3072]{1,0:T(8,128)S(1)} %get-tuple-element.62), kind=kOutput, calls=%fused_computation.14 | convolution fusion | flops 4847566848 | bytes 23592960 | tf_op jit(solution)/shard_map/dot_general | solution.py:632
  40.3 177.9 %reduce_update_gather.1 = (bf16[4,4,4,4,2,24,768]{6,5,4,3,2,1,0:T(8,128)(2,1)}, f32[3,2,6,3072]{3,2,1,0:T(8,128)}, f32[3,2,24,768]{3,2,1,0:T(8,128)}, f32[8,128]...) custom-call(f32[4,4,4,2,24,768]{5,4,3,2,1,0:T(8,128)} %bitcast.19, ...), custom_call_target="tpu_custom_call" | custom-call | tf_op jit(solution)/shard_map/reduce_update_gather/pallas_call | solution.py:605
  218.3 15.5 %place_outputs.1 = (bf16[4,4,2,24,3072]{4,3,2,1,0:T(8,128)(2,1)}, bf16[4,4,2,2,2,24,768]{6,5,4,3,2,1,0:T(8,128)(2,1)}, bf16[4,4,2,24,3072]{4,3,2,1,0:T(8,128)(2,...) custom-call(bf16[4,4,4,2,2,2,24,768]{7,6,5,4,3,2,1,0:T(8,128)(2,1)} , ...), custom_call_target="tpu_custom_call" | custom-call | tf_op jit(solution)/shard_map/place_outputs/pallas_call | solution.py:615
Async XLA Ops:
  1.9 14.7 %copy-start.1 = (bf16[3072,768]{1,0:T(8,128)(2,1)S(1)}, bf16[3072,768]{1,0:T(8,128)(2,1)}, u32[]{:S(2)}) copy-start(bf16[3072,768]{1,0:T(8,128)(2,1)} %refs_4_.1) | copy-start | bytes 14155780
  14.0 2.7 %copy-start = (bf16[1024,3072]{1,0:T(8,128)(2,1)}, bf16[1024,3072]{1,0:T(8,128)(2,1)S(1)}, u32[]{:S(2)}) copy-start(bf16[1024,3072]{1,0:T(8,128)(2,1)S(1)} %get-tuple-element.60.refs_9_) | copy-start | bytes 18874372
  16.7 5.0 %copy-start.2 = (bf16[768,3072]{1,0:T(8,128)(2,1)S(1)}, bf16[768,3072]{1,0:T(8,128)(2,1)}, u32[]{:S(2)}) copy-start(bf16[768,3072]{1,0:T(8,128)(2,1)} %refs_5_.1) | copy-start | bytes 14155780
  21.7 10.5 %copy-start.4 = (bf16[1024,768]{1,0:T(8,128)(2,1)}, bf16[1024,768]{1,0:T(8,128)(2,1)S(1)}, u32[]{:S(2)}) copy-start(bf16[1024,768]{1,0:T(8,128)(2,1)S(1)} %fusion.11.refs_2_) | copy-start | bytes 4718596
  21.7 10.5 %copy-start.3 = (bf16[1024,768]{1,0:T(8,128)(2,1)S(1)}, bf16[1024,768]{1,0:T(8,128)(2,1)}, u32[]{:S(2)}) copy-start(bf16[1024,768]{1,0:T(8,128)(2,1)} %refs_1_.1) | copy-start | bytes 4718596

commit v2 on v1

--- a/solution.py
+++ b/solution.py
@@ -18,6 +18,10 @@
 INV_ROOT_TAU = 1.0 / math.sqrt(2.0 * math.pi)
 
 MESH = pl.DeviceIdType.MESH
+UP1, DOWN1, UP2, DOWN2 = 0, 1, 2, 3
+UP, DOWN = 0, 1
+LAST, MIDDLE, EARLY = 0, 1, 2
+FAR, NEAR, PASS = 0, 1, 2
 STRIDES = (32, 8, 2)
 ORDERS = ((2, 1, 0), (1, 0, 2), (0, 2, 1))
 ROWS = 24
@@ -42,7 +46,7 @@
     states, refs = refs[:12], refs[12:]
     (lr_ref, clip_ref), refs = refs[:2], refs[2:]
     (w_out, up_out, down_out, norm_out, g_up1, g_down1, g_up2), refs = refs[:7], refs[7:]
-    (total, peer_in, rs1, rs2, rs3, norm_core, norm_axis, send_g, recv_g, send_w, recv_w, block_tmp, w_own, up_state, down_state), refs = refs[:15], refs[15:]
+    (total, peer_in, rs1, rs2, rs3, norm_line, norm_plane, send_g, recv_g, send_w, recv_w, block_tmp, w_own, up_state, down_state), refs = refs[:15], refs[15:]
     (left, flipped, mid_acc, mid_grad, w_tile, act_tile, der_tile, out_tile), refs = refs[:8], refs[8:]
     (load_sem, state_sem, pair_s, pair_r, rs1_s, rs1_r, rs2_s, rs2_r, rs3_s, rs3_r, nc_s, nc_r, na_s, na_r, xg_s, xg_r, xw_s, xw_r, own_sem, ag_s, ag_r, out_s, out_r) = refs[:23]
     row_sem, tile_sem, store_sem, pair_credit, ring_credit = refs[23:]
@@ -62,8 +66,10 @@
     def remote(src, dst, send_sem, recv_sem, target):
         return pltpu.make_async_remote_copy(src_ref=src, dst_ref=dst, send_sem=send_sem, recv_sem=recv_sem, device_id=(target,), device_id_type=MESH)
 
-    peers = [partner] + [device(axis, step(axis, hops)) for axis in range(COLOURS) for hops in (1, 2, 3)]
-    peers.append(me - member + lax.rem(member + 2, 4) + 1 - 2 * core)
+    line, plane = lax.rem(me, 8), me // 8
+    line_peers = [me - line + lax.rem(line + hops, 8) for hops in range(1, 8)]
+    plane_peers = [8 * lax.rem(plane + hops, 16) + line for hops in range(1, 16)]
+    peers = line_peers + plane_peers
     barrier = pltpu.get_barrier_semaphore()
     for peer in peers:
         pl.semaphore_signal(barrier, device_id=(peer,), device_id_type=MESH)
@@ -90,16 +96,15 @@
             place = (i // 16, lax.rem(i // SIDE, 4), lax.rem(i, SIDE))
             there = g_down1.at[pl.ds(pl.multiple_of(i * 2 * ROWS + (1 - core) * ROWS, 8), ROWS)]
             here = g_down1.at[pl.ds(pl.multiple_of(i * 2 * ROWS + core * ROWS, 8), ROWS)]
-            remote(there, peer_in.at[(pair_slot[1],) + place], pair_s.at[1, 0], pair_r.at[1, 0], partner).start()
-            pltpu.make_async_copy(here, total.at[(1,) + place], load_sem.at[1, 0]).start()
+            remote(there, peer_in.at[(pair_slot[DOWN1],) + place], pair_s.at[DOWN1, 0], pair_r.at[DOWN1, 0], partner).start()
+            pltpu.make_async_copy(here, total.at[(1,) + place], load_sem.at[DOWN1, 0]).start()
             return carry
 
         lax.fori_loop(low, high, move, 0)
 
-    loads[1] = [pltpu.make_async_copy(total.at[1], total.at[1], load_sem.at[1, 0])]
-    pairs[1] = [remote(peer_in.at[pair_slot[1]], peer_in.at[pair_slot[1]], pair_s.at[1, 0], pair_r.at[1, 0], partner)]
-    loads[3] = [pltpu.make_async_copy(g_down2.at[:, :, :, core], total.at[3], load_sem.at[3, 0])]
-    loads[3][0].start()
+    loads[DOWN1] = [pltpu.make_async_copy(total.at[1], total.at[1], load_sem.at[DOWN1, 0])]
+    pairs[DOWN1] = [remote(peer_in.at[pair_slot[DOWN1]], peer_in.at[pair_slot[DOWN1]], pair_s.at[DOWN1, 0], pair_r.at[DOWN1, 0], partner)]
+    loads[DOWN2] = [pltpu.make_async_copy(g_down2.at[:, :, :, core], total.at[3], load_sem.at[DOWN2, 0])]
 
     tiles = SIDE * lanes // TILE
 
@@ -114,9 +119,11 @@
         ]
 
     def fetch_b(t, slot):
+        return [pltpu.make_async_copy(act1.at[:, span(t)], act_tile.at[slot], tile_sem.at[slot, 1])]
+
+    def fetch_c(t, slot):
         return [
             pltpu.make_async_copy(w_down1.at[span(t)], w_tile.at[slot], tile_sem.at[slot, 0]),
-            pltpu.make_async_copy(act1.at[:, span(t)], act_tile.at[slot], tile_sem.at[slot, 1]),
             pltpu.make_async_copy(der1.at[:, span(t)], der_tile.at[slot], tile_sem.at[slot, 2]),
         ]
 
@@ -131,6 +138,7 @@
     row_loads = [pltpu.make_async_copy(grad_rows, left, row_sem.at[0]), pltpu.make_async_copy(mid_rows, mid_grad, row_sem.at[1])]
     begin(row_loads)
     begin(fetch_a(0, 0))
+    begin(loads[DOWN2])
     state_loads = []
     for field in range(COLOURS):
         for mat in range(SIDE):
@@ -138,13 +146,13 @@
             state_loads.append(pltpu.make_async_copy(states[4 * field + mat], dst, state_sem.at[field, mat]))
     begin(state_loads)
     def store_a(t, slot):
-        return [pltpu.make_async_copy(out_tile.at[slot], g_up2.at[:, :, :, :, span(t)], store_sem.at[slot, 0])]
+        return [pltpu.make_async_copy(out_tile.at[slot], g_up2.at[:, :, :, :, span(t)], store_sem.at[slot])]
 
     def store_b(t, slot):
-        return [
-            pltpu.make_async_copy(out_tile.at[slot], g_up1.at[:, :, :, :, span(t)], store_sem.at[slot, 0]),
-            pltpu.make_async_copy(mid_acc.at[slot], g_down1.at[span(t)], store_sem.at[slot, 1]),
-        ]
+        return [pltpu.make_async_copy(mid_acc.at[slot], g_down1.at[span(t)], store_sem.at[slot])]
+
+    def store_c(t, slot):
+        return [pltpu.make_async_copy(out_tile.at[slot], g_up1.at[:, :, :, :, span(t)], store_sem.at[slot])]
 
     def run(first, last, fetch, store, work):
         def tile(t, carry):
@@ -179,20 +187,19 @@
 
     def work_b(slot):
         mid_acc[slot] = dot(act_tile[slot], mid_grad[...], 0, 0)
+
+    def work_c(slot):
         grad_act1 = dot(mid_grad[...], w_tile[slot], 1, 1).astype(jnp.bfloat16)
         grad_pre1 = (grad_act1.astype(jnp.float32) * der_tile[slot]).astype(jnp.bfloat16)
         out_tile[slot] = dot(flipped[...], grad_pre1, 1, 0).reshape(out_tile.shape[1:])
 
-    end(row_loads)
-    flipped[...] = mid_grad[...].T
-    mid_acc[...] = jnp.zeros_like(mid_acc)
-    run(0, 1, fetch_a, store_a, work_a)
     pl.semaphore_wait(barrier, len(peers))
-    pairs[3] = [remote(g_down2.at[:, :, :, 1 - core], peer_in.at[pair_slot[3]], pair_s.at[3, 0], pair_r.at[3, 0], partner)]
-    pairs[3][0].start()
+    pairs[DOWN2] = [remote(g_down2.at[:, :, :, 1 - core], peer_in.at[pair_slot[DOWN2]], pair_s.at[DOWN2, 0], pair_r.at[DOWN2, 0], partner)]
+    pairs[DOWN2][0].start()
 
     def part(mats, coords, colour, side):
-        index = [mats, ALL, ALL, ALL, pl.ds(CHUNK * colour, CHUNK), pl.ds(half * side, half)]
+        lane = ALL if side is None else pl.ds(half * side, half)
+        index = [mats, ALL, ALL, ALL, pl.ds(CHUNK * colour, CHUNK), lane]
         for axis, coord in coords.items():
             index[1 + axis] = coord
         return tuple(index)
@@ -239,24 +246,24 @@
             for colour in range(COLOURS):
                 for side in range(SIDES):
                     coord, target = self.near(colour, side)
-                    self.copies[colour, side, 0].wait_recv()
+                    self.copies[colour, side, FAR].wait_recv()
 
                     def add_own(i, carry, colour=colour, side=side, coord=coord):
-                        self.buf[colour, side, 0, i] = self.buf[colour, side, 0, i] + total[self.row(colour, coord, side, i)]
+                        self.buf[colour, side, FAR, i] = self.buf[colour, side, FAR, i] + total[self.row(colour, coord, side, i)]
                         return carry
 
                     lax.fori_loop(0, self.count, add_own, 0)
-                    self.send(colour, side, 2, self.buf.at[colour, side, 0], target)
+                    self.send(colour, side, 2, self.buf.at[colour, side, FAR], target)
 
         def finish(self):
             for colour in range(COLOURS):
                 for side in range(SIDES):
-                    self.copies[colour, 1 - side, 1].wait_recv()
-                    self.copies[colour, side, 2].wait_recv()
+                    self.copies[colour, 1 - side, NEAR].wait_recv()
+                    self.copies[colour, side, PASS].wait_recv()
 
                     def add_both(i, carry, colour=colour, side=side):
                         own = self.row(colour, pos[ORDERS[colour][self.level]], side, i)
-                        total[own] = total[own] + (self.buf[colour, 1 - side, 1, i] + self.buf[colour, side, 2, i])
+                        total[own] = total[own] + (self.buf[colour, 1 - side, NEAR, i] + self.buf[colour, side, PASS, i])
                         return carry
 
                     lax.fori_loop(0, self.count, add_both, 0)
@@ -266,6 +273,39 @@
                 copy.wait_send()
 
     ring_slot = (1, 0, 1, 0)
+    class Direct:
+        def __init__(self, base, buf, send_sem, recv_sem):
+            self.base, self.buf, self.send_sem, self.recv_sem = base, buf, send_sem, recv_sem
+            self.copies = {}
+
+        def index(self, colour, coord, mats):
+            coords = {axis: pos[axis] for axis in range(COLOURS)}
+            coords[ORDERS[colour][2]] = coord
+            return part(mats, coords, colour, None)
+
+        def start(self):
+            for hops in (2, 1, 3):
+                for colour in range(COLOURS):
+                    axis = ORDERS[colour][2]
+                    coord = step(axis, hops)
+                    spots = (colour, hops - 1)
+                    src = total.at[self.index(colour, coord, slice(self.base, self.base + 2))]
+                    copy = remote(src, self.buf.at[spots], self.send_sem.at[spots], self.recv_sem.at[spots], device(axis, coord))
+                    copy.start()
+                    self.copies[spots] = copy
+
+        def finish(self):
+            for colour in range(COLOURS):
+                for hops in range(COLOURS):
+                    self.copies[colour, hops].wait_recv()
+                for mat in range(SIDES):
+                    own = self.index(colour, pos[ORDERS[colour][2]], self.base + mat)
+                    total[own] = (total[own] + self.buf[colour, 0, mat]) + (self.buf[colour, 1, mat] + self.buf[colour, 2, mat])
+
+        def drain(self):
+            for copy in self.copies.values():
+                copy.wait_send()
+
     first = {mat: Phase(0, mat, rs1.at[ring_slot[mat]], rs1_s.at[mat], rs1_r.at[mat]) for mat in mat_order}
 
     def add_pair(mat):
@@ -290,59 +330,61 @@
             pl.semaphore_signal(ring_credit.at[ring_slot[mat]], device_id=(peer,), device_id_type=MESH)
 
     second = {base: Phase(1, base, rs2.at[base // 2], rs2_s.at[base // 2], rs2_r.at[base // 2]) for base in (2, 0)}
-    third = {base: Phase(2, base, rs3.at[base // 2], rs3_s.at[base // 2], rs3_r.at[base // 2]) for base in (2, 0)}
-    run(1, 4, fetch_a, store_a, work_a)
-    add_pair(3)
-    first[3].start()
-    issue_up(2, 0)
-    run(4, tiles, fetch_a, store_a, work_a)
-    issue_up(2, 1)
-    begin(fetch_b(0, 0))
+    third = {base: Direct(base, rs3.at[base // 2], rs3_s.at[base // 2], rs3_r.at[base // 2]) for base in (2, 0)}
+    end(row_loads)
+    flipped[...] = mid_grad[...].T
+    mid_acc[...] = jnp.zeros_like(mid_acc)
+    run(0, 3, fetch_a, store_a, work_a)
+    add_pair(DOWN2)
+    first[DOWN2].start()
+    issue_up(UP2, 0)
+    run(3, tiles, fetch_a, store_a, work_a)
+    issue_up(UP2, 1)
+    begin(fetch_b(0, 0) + fetch_c(0, 0))
     in_load = pltpu.make_async_copy(in_rows, left, row_sem.at[0])
     in_load.start()
-    first[3].forward()
     mid_grad[...] = mid_acc[...].reshape(mid_grad.shape).astype(jnp.bfloat16)
+    first[DOWN2].forward()
+    run(0, 3, fetch_b, store_b, work_b)
+    add_pair(UP2)
+    first[UP2].start()
+    run(3, tiles, fetch_b, store_b, work_b)
+    pl.semaphore_wait(pair_credit)
+    issue_rows(0, 64)
     in_load.wait()
     flipped[...] = left[...].T
-    run(0, 2, fetch_b, store_b, work_b)
-    add_pair(2)
-    first[2].start()
-    run(2, 4, fetch_b, store_b, work_b)
-    first[2].forward()
-    pl.semaphore_wait(pair_credit, 1)
-    issue_rows(0, 32)
-    pl.semaphore_wait(pair_credit, 1)
-    issue_up(0, 0)
-    close(3)
-    run(4, tiles, fetch_b, store_b, work_b)
-    issue_rows(32, 64)
-    issue_up(0, 1)
-    close(2)
-    second[2].start()
-    add_pair(1)
+    close(DOWN2)
+    run(0, 2, fetch_c, store_c, work_c)
+    first[UP2].forward()
+    run(2, 4, fetch_c, store_c, work_c)
+    add_pair(DOWN1)
     pl.semaphore_wait(ring_credit.at[0], len(ring))
-    first[1].start()
-    second[2].forward()
-    add_pair(0)
+    first[DOWN1].start()
+    pl.semaphore_wait(pair_credit)
+    issue_up(UP1, 0)
+    run(4, tiles, fetch_c, store_c, work_c)
+    issue_up(UP1, 1)
+    close(UP2)
+    second[UP2].start()
+    add_pair(UP1)
     pl.semaphore_wait(ring_credit.at[1], len(ring))
-    first[0].start()
-    second[2].finish()
-    third[2].start()
-    first[1].forward()
-    third[2].forward()
-    first[1].finish()
-    third[2].finish()
-    first[0].forward()
-    first[0].finish()
-    second[0].start()
-    second[0].forward()
-    second[0].finish()
-    third[0].start()
-    third[0].forward()
-    third[0].finish()
+    first[UP1].start()
+    first[DOWN1].forward()
+    second[UP2].forward()
+    second[UP2].finish()
+    third[UP2].start()
+    first[UP1].forward()
+    first[DOWN1].finish()
+    third[UP2].finish()
+    first[UP1].finish()
+    second[UP1].start()
+    second[UP1].forward()
+    second[UP1].finish()
+    third[UP1].start()
+    third[UP1].finish()
 
     group_scale = 1.0 / 128.0
-    grad_own = [total[mat, pos[0], pos[1], pos[2]] * group_scale for mat in range(SIDE)]
+    grad_own = [total[mat, *pos] * group_scale for mat in range(SIDE)]
     partial = None
     for block in grad_own:
         square = block * block
@@ -350,9 +392,17 @@
             for col in range(max(1, lanes // 128)):
                 tile = square[8 * row:8 * row + 8, 128 * col:128 * col + 128]
                 partial = tile if partial is None else partial + tile
-    norm_core[core] = partial
-    swap = remote(norm_core.at[core], norm_core.at[core], nc_s.at[0], nc_r.at[0], partner)
-    swap.start()
+    norm_line[line] = partial
+    sends = []
+
+    def spread(buf, slot, targets, send_sem, recv_sem):
+        copies = []
+        for i, target in enumerate(targets):
+            copies.append(remote(buf.at[slot], buf.at[slot], send_sem.at[i], recv_sem.at[i], target))
+            copies[i].start()
+        return copies
+
+    swap = spread(norm_line, line, line_peers, nc_s, nc_r)
     for target in range(SIDE):
         for i, mat in enumerate((0, 2)):
             send_g[target, i] = grad_own[mat][SUB * target:SUB * target + SUB]
@@ -363,21 +413,14 @@
         copy.start()
         moves.append(copy)
     recv_g[member] = send_g[member]
-    swap.wait_recv()
-    running = norm_core[0] + norm_core[1]
-    sends = [swap] + moves
-    for axis in (2, 1, 0):
-        norm_axis[axis, pos[axis]] = running
-        copies = []
-        for hops in (1, 2, 3):
-            coord = step(axis, hops)
-            copy = remote(norm_axis.at[axis, pos[axis]], norm_axis.at[axis, pos[axis]], na_s.at[axis, hops - 1], na_r.at[axis, hops - 1], device(axis, coord))
-            copy.start()
-            copies.append(copy)
-        for copy in copies:
-            copy.wait_recv()
-        sends = sends + copies
-        running = (norm_axis[axis, 0] + norm_axis[axis, 1]) + (norm_axis[axis, 2] + norm_axis[axis, 3])
+    for copy in swap:
+        copy.wait_recv()
+    norm_plane[plane] = jnp.sum(norm_line[...], axis=0)
+    cross = spread(norm_plane, plane, plane_peers, na_s, na_r)
+    for copy in cross:
+        copy.wait_recv()
+    running = jnp.sum(norm_plane[...], axis=0)
+    sends = swap + cross + moves
     norm = jnp.sqrt(jnp.sum(jnp.sum(running, axis=1, keepdims=True), axis=0, keepdims=True))
     norm_out[...] = jnp.broadcast_to(norm, norm_out.shape)
     clip_scale = jnp.minimum(1.0, clip_ref[0] / (norm + NORM_EPS))
@@ -426,43 +469,51 @@
             copy.start()
             handed.append(copy)
 
+        def start_direct(self):
+            for hops in (2, 1, 3):
+                for colour in range(COLOURS):
+                    axis = ORDERS[colour][self.level]
+                    dst = self.spot(colour, pos[axis], None)
+                    src = w_own.at[pl.ds(2 * self.group, 2), pl.ds(CHUNK * colour, CHUNK)] if self.level == 2 else dst
+                    spots = (self.group, self.level, colour, 0, hops - 1)
+                    copy = remote(src, dst, ag_s.at[spots], ag_r.at[spots], device(axis, step(axis, hops)))
+                    copy.start()
+                    self.copies[colour, hops] = copy
+
+        def finish_direct(self):
+            for copy in self.copies.values():
+                copy.wait_recv()
+
         def start(self):
             for kind in range(SIDES):
                 for colour in range(COLOURS):
                     for side in range(SIDES):
-                        lane_side = side if kind == 0 else 1 - side
-                        dst = self.spot(colour, pos[ORDERS[colour][self.level]], lane_side)
-                        src = dst
-                        if self.level == 2:
-                            src = w_own.at[pl.ds(2 * self.group, 2), pl.ds(CHUNK * colour, CHUNK), pl.ds(half * lane_side, half)]
-                        self.send(colour, side, kind, src, dst)
-            if self.level == 0:
-                for colour in range(COLOURS):
-                    self.hand(self.spot(colour, pos[ORDERS[colour][0]], None), 5 * colour)
+                        ref = self.spot(colour, pos[ORDERS[colour][0]], side if kind == 0 else 1 - side)
+                        self.send(colour, side, kind, ref, ref)
+            for colour in range(COLOURS):
+                self.hand(self.spot(colour, pos[ORDERS[colour][0]], None), 5 * colour)
 
         def forward(self):
             for colour in range(COLOURS):
                 for side in range(SIDES):
-                    self.copies[colour, side, 0].wait_recv()
+                    self.copies[colour, side, FAR].wait_recv()
                     ref = self.spot(colour, self.near(colour, 1 - side)[0], side)
                     self.send(colour, side, 2, ref, ref)
 
         def finish(self):
             for colour in range(COLOURS):
                 for side in range(SIDES):
-                    self.copies[colour, side, 1].wait_recv()
-                    if self.level == 0:
-                        self.hand(self.spot(colour, self.near(colour, 1 - side)[0], None), 5 * colour + 1 + side)
+                    self.copies[colour, side, NEAR].wait_recv()
+                    self.hand(self.spot(colour, self.near(colour, 1 - side)[0], None), 5 * colour + 1 + side)
             for colour in range(COLOURS):
                 for side in range(SIDES):
-                    self.copies[colour, side, 2].wait_recv()
-                    if self.level == 0:
-                        self.hand(self.spot(colour, step(ORDERS[colour][0], 2), side), 5 * colour + 3 + side)
-
-    keeps = [pltpu.make_async_copy(w_own.at[pl.ds(2 * group, 2)], w_out.at[pl.ds(2 * group, 2), pos[0], pos[1], pos[2], core], own_sem.at[group]) for group in range(SIDES)]
+                    self.copies[colour, side, PASS].wait_recv()
+                    self.hand(self.spot(colour, step(ORDERS[colour][0], 2), side), 5 * colour + 3 + side)
+
+    keeps = [pltpu.make_async_copy(w_own.at[pl.ds(2 * group, 2)], w_out.at[pl.ds(2 * group, 2), *pos, core], own_sem.at[group]) for group in range(SIDES)]
     gathers = {(group, level): Gather(group, level) for group in range(SIDES) for level in range(COLOURS)}
-    gathers[1, 2].start()
-    keeps[1].start()
+    gathers[DOWN, EARLY].start_direct()
+    keeps[DOWN].start()
 
     for copy in moves:
         copy.wait_recv()
@@ -483,7 +534,9 @@
     recv_w[member] = send_w[member]
     state_stores = [pltpu.make_async_copy(up_state, up_out, state_sem.at[0, 0]), pltpu.make_async_copy(down_state, down_out, state_sem.at[0, 1])]
     begin(state_stores)
-    gathers[1, 2].forward()
+    gathers[DOWN, EARLY].finish_direct()
+    keeps[DOWN].wait()
+    gathers[DOWN, MIDDLE].start_direct()
     for copy in moves:
         copy.wait_recv()
     sends = sends + moves
@@ -491,28 +544,22 @@
         for source in range(SIDE):
             block_tmp[SUB * source:SUB * source + SUB] = recv_w[source, i]
         w_own[i] = block_tmp[...].astype(jnp.bfloat16)
-    gathers[0, 2].start()
-    keeps[0].start()
-    gathers[1, 2].finish()
-    keeps[1].wait()
-    gathers[1, 1].start()
-    gathers[0, 2].forward()
-    gathers[1, 1].forward()
-    gathers[0, 2].finish()
-    keeps[0].wait()
-    gathers[0, 1].start()
-    gathers[1, 1].finish()
-    gathers[1, 0].start()
-    gathers[0, 1].forward()
-    gathers[0, 1].finish()
-    gathers[0, 0].start()
-    gathers[1, 0].forward()
-    gathers[0, 0].forward()
-    gathers[1, 0].finish()
-    gathers[0, 0].finish()
+    gathers[UP, EARLY].start_direct()
+    keeps[UP].start()
+    gathers[DOWN, MIDDLE].finish_direct()
+    gathers[DOWN, LAST].start()
+    gathers[UP, EARLY].finish_direct()
+    keeps[UP].wait()
+    gathers[UP, MIDDLE].start_direct()
+    gathers[UP, MIDDLE].finish_direct()
+    gathers[UP, LAST].start()
+    gathers[DOWN, LAST].forward()
+    gathers[DOWN, LAST].finish()
+    gathers[UP, LAST].forward()
+    gathers[UP, LAST].finish()
     for gather in gathers.values():
         sends = sends + list(gather.copies.values())
-    for phase in [first[1], first[0]] + list(second.values()) + list(third.values()):
+    for phase in [first[DOWN1], first[UP1]] + list(second.values()) + list(third.values()):
         phase.drain()
     for mat in mat_order:
         for copy in pairs[mat]:
@@ -577,9 +624,9 @@
         pltpu.VMEM((SIDES, SIDE, SIDE, SIDE, ROWS, lanes), f32),
         pltpu.VMEM((SIDES, COLOURS, SIDES, COLOURS, SIDE, SIDE, CHUNK, half), f32),
         pltpu.VMEM((SIDES, COLOURS, SIDES, COLOURS, SIDES, SIDE, CHUNK, half), f32),
-        pltpu.VMEM((SIDES, COLOURS, SIDES, COLOURS, SIDES, CHUNK, half), f32),
-        pltpu.VMEM((2, 8, min(lanes, 128)), f32),
-        pltpu.VMEM((3, 4, 8, min(lanes, 128)), f32),
+        pltpu.VMEM((SIDES, COLOURS, COLOURS, SIDES, CHUNK, lanes), f32),
+        pltpu.VMEM((8, 8, 128), f32),
+        pltpu.VMEM((16, 8, 128), f32),
         pltpu.VMEM((SIDE, SIDES, SUB, lanes), f32),
         pltpu.VMEM((SIDE, SIDES, SUB, lanes), f32),
         pltpu.VMEM((SIDE, SIDES, SUB, lanes), f32),
@@ -597,10 +644,10 @@
         pltpu.VMEM((SIDES, local_rows, TILE), f32),
         pltpu.VMEM((SIDES, SIDE, SIDE, SIDES, ROWS, TILE), f32),
         dma((SIDE, SIDE)), dma((COLOURS, SIDE)), dma((SIDE, SIDE)), dma((SIDE, SIDE)),
-        dma((SIDE, COLOURS, SIDES, COLOURS)), dma((SIDE, COLOURS, SIDES, COLOURS)), dma((SIDES, COLOURS, SIDES, COLOURS)), dma((SIDES, COLOURS, SIDES, COLOURS)), dma((SIDES, COLOURS, SIDES, COLOURS)), dma((SIDES, COLOURS, SIDES, COLOURS)),
-        dma((1,)), dma((1,)), dma((COLOURS, COLOURS)), dma((COLOURS, COLOURS)), dma((COLOURS,)), dma((COLOURS,)), dma((COLOURS,)), dma((COLOURS,)),
+        dma((SIDE, COLOURS, SIDES, COLOURS)), dma((SIDE, COLOURS, SIDES, COLOURS)), dma((SIDES, COLOURS, SIDES, COLOURS)), dma((SIDES, COLOURS, SIDES, COLOURS)), dma((SIDES, COLOURS, COLOURS)), dma((SIDES, COLOURS, COLOURS)),
+        dma((7,)), dma((7,)), dma((15,)), dma((15,)), dma((COLOURS,)), dma((COLOURS,)), dma((COLOURS,)), dma((COLOURS,)),
         dma((SIDES,)), dma((SIDES, COLOURS, COLOURS, SIDES, COLOURS)), dma((SIDES, COLOURS, COLOURS, SIDES, COLOURS)), dma((SIDES, 15)), dma((SIDES, 15)),
-        dma((SIDES,)), dma((SIDES, COLOURS)), dma((SIDES, SIDES)), pltpu.SemaphoreType.REGULAR, pltpu.SemaphoreType.REGULAR((2,)),
+        dma((SIDES,)), dma((SIDES, COLOURS)), dma((SIDES,)), pltpu.SemaphoreType.REGULAR, pltpu.SemaphoreType.REGULAR((2,)),
     ]
     outs = pl.pallas_call(
         functools.partial(comm_kernel, lanes),

time: 234 us -> 224 us (0.957)
  Pallas kernels: 193 us -> 183 us
    pallas_call x1, Pallas kernels: 178 us -> 168 us  [comm_call(): pl.pallas_call(functools.partial(comm_kernel, lanes), name='reduce_update...]
where the time goes in v2:
time: 224 us
  Pallas kernels  183 us (82%)
  matrix products  35.7 us (16%)
  local copies, waits for them, and re-layouts  2.67 us (1%)
    pallas_call x1, Pallas kernels, comm_call(): pl.pallas_call(functools.partial(comm_kernel, lanes), name='reduce_update...  168 us
    pallas_call x1, Pallas kernels, comm_call(): pl.pallas_call(functools.partial(place_kernel, lanes), name='place_output...  15.5 us
    dot_general x1, matrix products, shard_body(): jnp.dot(act_in, w_up1, preferred_element_type=jnp.float32)  12 us
    dot_general x1, matrix products, shard_body(): jnp.dot(mid_act, w_up2, preferred_element_type=jnp.float32)  10.5 us
    dot_general x1, matrix products, mat_tn(): lax.dot_general(left, right, (((0,), (0,)), ((), ())), preferred_element_...  8.14 us
    dot_general x1, matrix products, shard_body(): jnp.dot(act_up1, w_down1, preferred_element_type=jnp.float32)  5.02 us

profile of v2, /device:TPU:1, one launch (start us, length us, event | category | flops | bytes accessed | tf_op | source)
XLA Modules:
  0.0 224.0 jit_solution(8303895415296783058)
XLA Ops:
  1.9 0.0 copy-start.1
  2.0 12.0 %fusion.3 = (f32[1024,3072]{1,0:T(8,128)}, bf16[1024,3072]{1,0:T(8,128)(2,1)S(1)}) fusion(bf16[1024,768]{1,0:T(8,128)(2,1)} %refs_3_.1, bf16[768,3072]{1,0:T(8,128)(2,1)} %param.22), kind=kOutput, calls=%fused_computation.5 | convolution fusion | flops 4863295488 | bytes 25165824 | tf_op jit(solution)/shard_map/dot_general | solution.py:694
  14.0 0.0 copy-start
  14.0 2.6 %copy-done = bf16[1024,3072]{1,0:T(8,128)(2,1)} copy-done((bf16[1024,3072]{1,0:T(8,128)(2,1)}, bf16[1024,3072]{1,0:T(8,128)(2,1)S(1)}, u32[]{:S(2)}) %copy-start) | copy-done | bytes 6291480
  16.7 0.0 copy-done.1
  16.7 0.0 copy-start.2
  16.7 5.0 %fusion.11.refs_2_ = bf16[1024,768]{1,0:T(8,128)(2,1)S(1)} fusion(bf16[1024,3072]{1,0:T(8,128)(2,1)S(1)} %get-tuple-element.60.refs_9_, bf16[3072,768]{1,0:T(8,128)(2,1)S(1)} %copy-done.1), kind=kOutput, calls=%fused_computation.17 | convolution fusion | flops 4831838208 | bytes 12582912 | tf_op jit(solution)/shard_map/dot_general | solution.py:696
  21.7 0.0 copy-done.2
  21.7 0.0 copy-start.4
  21.7 0.0 copy-start.3
  21.7 10.5 %fusion.7 = (f32[1024,3072]{1,0:T(8,128)}, f32[1024,3072]{1,0:T(8,128)S(1)}) fusion(bf16[1024,768]{1,0:T(8,128)(2,1)S(1)} %fusion.11.refs_2_, bf16[768,3072]{1,0:T(8,128)(2,1)S(1)} %copy-done.2), kind=kOutput, calls=%fused_computation.9 | convolution fusion | flops 4857004032 | bytes 31457280 | tf_op jit(solution)/shard_map/dot_general | solution.py:697
  32.2 0.0 copy-done.4
  32.2 0.0 copy-done.3
  32.2 8.1 %fusion.8 = f32[3072,768]{1,0:T(8,128)} fusion(bf16[1024,768]{1,0:T(8,128)(2,1)S(1)} %copy-done.3, f32[1024,3072]{1,0:T(8,128)S(1)} %get-tuple-element.62), kind=kOutput, calls=%fused_computation.14 | convolution fusion | flops 4847566848 | bytes 23592960 | tf_op jit(solution)/shard_map/dot_general | solution.py:679
  40.3 167.9 %reduce_update_gather.1 = (bf16[4,4,4,4,2,24,768]{6,5,4,3,2,1,0:T(8,128)(2,1)}, f32[3,2,6,3072]{3,2,1,0:T(8,128)}, f32[3,2,24,768]{3,2,1,0:T(8,128)}, f32[8,128]...) custom-call(f32[4,4,4,2,24,768]{5,4,3,2,1,0:T(8,128)} %bitcast.19, ...), custom_call_target="tpu_custom_call" | custom-call | tf_op jit(solution)/shard_map/reduce_update_gather/pallas_call | solution.py:652
  208.3 15.5 %place_outputs.1 = (bf16[4,4,2,24,3072]{4,3,2,1,0:T(8,128)(2,1)}, bf16[4,4,2,2,2,24,768]{6,5,4,3,2,1,0:T(8,128)(2,1)}, bf16[4,4,2,24,3072]{4,3,2,1,0:T(8,128)(2,...) custom-call(bf16[4,4,4,2,2,2,24,768]{7,6,5,4,3,2,1,0:T(8,128)(2,1)} , ...), custom_call_target="tpu_custom_call" | custom-call | tf_op jit(solution)/shard_map/place_outputs/pallas_call | solution.py:662
Async XLA Ops:
  1.9 14.7 %copy-start.1 = (bf16[3072,768]{1,0:T(8,128)(2,1)S(1)}, bf16[3072,768]{1,0:T(8,128)(2,1)}, u32[]{:S(2)}) copy-start(bf16[3072,768]{1,0:T(8,128)(2,1)} %refs_4_.1) | copy-start | bytes 14155780
  14.0 2.7 %copy-start = (bf16[1024,3072]{1,0:T(8,128)(2,1)}, bf16[1024,3072]{1,0:T(8,128)(2,1)S(1)}, u32[]{:S(2)}) copy-start(bf16[1024,3072]{1,0:T(8,128)(2,1)S(1)} %get-tuple-element.60.refs_9_) | copy-start | bytes 18874372
  16.7 5.0 %copy-start.2 = (bf16[768,3072]{1,0:T(8,128)(2,1)S(1)}, bf16[768,3072]{1,0:T(8,128)(2,1)}, u32[]{:S(2)}) copy-start(bf16[768,3072]{1,0:T(8,128)(2,1)} %refs_5_.1) | copy-start | bytes 14155780
  21.7 10.5 %copy-start.4 = (bf16[1024,768]{1,0:T(8,128)(2,1)}, bf16[1024,768]{1,0:T(8,128)(2,1)S(1)}, u32[]{:S(2)}) copy-start(bf16[1024,768]{1,0:T(8,128)(2,1)S(1)} %fusion.11.refs_2_) | copy-start | bytes 4718596
  21.7 10.5 %copy-start.3 = (bf16[1024,768]{1,0:T(8,128)(2,1)S(1)}, bf16[1024,768]{1,0:T(8,128)(2,1)}, u32[]{:S(2)}) copy-start(bf16[1024,768]{1,0:T(8,128)(2,1)} %refs_1_.1) | copy-start | bytes 4718596

commit v3 on v2

--- a/solution.py
+++ b/solution.py
@@ -193,10 +193,6 @@
         grad_pre1 = (grad_act1.astype(jnp.float32) * der_tile[slot]).astype(jnp.bfloat16)
         out_tile[slot] = dot(flipped[...], grad_pre1, 1, 0).reshape(out_tile.shape[1:])
 
-    pl.semaphore_wait(barrier, len(peers))
-    pairs[DOWN2] = [remote(g_down2.at[:, :, :, 1 - core], peer_in.at[pair_slot[DOWN2]], pair_s.at[DOWN2, 0], pair_r.at[DOWN2, 0], partner)]
-    pairs[DOWN2][0].start()
-
     def part(mats, coords, colour, side):
         lane = ALL if side is None else pl.ds(half * side, half)
         index = [mats, ALL, ALL, ALL, pl.ds(CHUNK * colour, CHUNK), lane]
@@ -334,18 +330,22 @@
     end(row_loads)
     flipped[...] = mid_grad[...].T
     mid_acc[...] = jnp.zeros_like(mid_acc)
-    run(0, 3, fetch_a, store_a, work_a)
+    run(0, 2, fetch_a, store_a, work_a)
+    pl.semaphore_wait(barrier, len(peers))
+    pairs[DOWN2] = [remote(g_down2.at[:, :, :, 1 - core], peer_in.at[pair_slot[DOWN2]], pair_s.at[DOWN2, 0], pair_r.at[DOWN2, 0], partner)]
+    pairs[DOWN2][0].start()
+    run(2, 5, fetch_a, store_a, work_a)
+    issue_up(UP2, 0)
     add_pair(DOWN2)
     first[DOWN2].start()
-    issue_up(UP2, 0)
-    run(3, tiles, fetch_a, store_a, work_a)
+    run(5, tiles, fetch_a, store_a, work_a)
     issue_up(UP2, 1)
     begin(fetch_b(0, 0) + fetch_c(0, 0))
     in_load = pltpu.make_async_copy(in_rows, left, row_sem.at[0])
     in_load.start()
     mid_grad[...] = mid_acc[...].reshape(mid_grad.shape).astype(jnp.bfloat16)
+    run(0, 3, fetch_b, store_b, work_b)
     first[DOWN2].forward()
-    run(0, 3, fetch_b, store_b, work_b)
     add_pair(UP2)
     first[UP2].start()
     run(3, tiles, fetch_b, store_b, work_b)
@@ -353,16 +353,15 @@
     issue_rows(0, 64)
     in_load.wait()
     flipped[...] = left[...].T
+    run(0, 3, fetch_c, store_c, work_c)
     close(DOWN2)
-    run(0, 2, fetch_c, store_c, work_c)
     first[UP2].forward()
-    run(2, 4, fetch_c, store_c, work_c)
+    pl.semaphore_wait(pair_credit)
+    issue_up(UP1, 0)
     add_pair(DOWN1)
     pl.semaphore_wait(ring_credit.at[0], len(ring))
     first[DOWN1].start()
-    pl.semaphore_wait(pair_credit)
-    issue_up(UP1, 0)
-    run(4, tiles, fetch_c, store_c, work_c)
+    run(3, tiles, fetch_c, store_c, work_c)
     issue_up(UP1, 1)
     close(UP2)
     second[UP2].start()
@@ -371,13 +370,13 @@
     first[UP1].start()
     first[DOWN1].forward()
     second[UP2].forward()
+    first[UP1].forward()
     second[UP2].finish()
     third[UP2].start()
-    first[UP1].forward()
     first[DOWN1].finish()
-    third[UP2].finish()
     first[UP1].finish()
     second[UP1].start()
+    third[UP2].finish()
     second[UP1].forward()
     second[UP1].finish()
     third[UP1].start()

time: 224 us -> 224 us (level)
  no operation moved by 1% of the time
where the time goes in v3:
time: 224 us
  Pallas kernels  183 us (82%)
  matrix products  35.7 us (16%)
  local copies, waits for them, and re-layouts  2.67 us (1%)
    pallas_call x1, Pallas kernels, comm_call(): pl.pallas_call(functools.partial(comm_kernel, lanes), name='reduce_update...  168 us
    pallas_call x1, Pallas kernels, comm_call(): pl.pallas_call(functools.partial(place_kernel, lanes), name='place_output...  15.5 us
    dot_general x1, matrix products, shard_body(): jnp.dot(act_in, w_up1, preferred_element_type=jnp.float32)  12 us
    dot_general x1, matrix products, shard_body(): jnp.dot(mid_act, w_up2, preferred_element_type=jnp.float32)  10.5 us
    dot_general x1, matrix products, mat_tn(): lax.dot_general(left, right, (((0,), (0,)), ((), ())), preferred_element_...  8.14 us
    dot_general x1, matrix products, shard_body(): jnp.dot(act_up1, w_down1, preferred_element_type=jnp.float32)  5.02 us

profile of v3, /device:TPU:1, one launch (start us, length us, event | category | flops | bytes accessed | tf_op | source)
XLA Modules:
  0.0 223.9 jit_solution(16045435615160694570)
XLA Ops:
  1.9 0.0 copy-start.1
  2.0 12.0 %fusion.3 = (f32[1024,3072]{1,0:T(8,128)}, bf16[1024,3072]{1,0:T(8,128)(2,1)S(1)}) fusion(bf16[1024,768]{1,0:T(8,128)(2,1)} %refs_3_.1, bf16[768,3072]{1,0:T(8,128)(2,1)} %param.22), kind=kOutput, calls=%fused_computation.5 | convolution fusion | flops 4863295488 | bytes 25165824 | tf_op jit(solution)/shard_map/dot_general | solution.py:693
  14.0 0.0 copy-start
  14.0 2.6 %copy-done = bf16[1024,3072]{1,0:T(8,128)(2,1)} copy-done((bf16[1024,3072]{1,0:T(8,128)(2,1)}, bf16[1024,3072]{1,0:T(8,128)(2,1)S(1)}, u32[]{:S(2)}) %copy-start) | copy-done | bytes 6291480
  16.7 0.0 copy-done.1
  16.7 0.0 copy-start.2
  16.7 5.0 %fusion.11.refs_2_ = bf16[1024,768]{1,0:T(8,128)(2,1)S(1)} fusion(bf16[1024,3072]{1,0:T(8,128)(2,1)S(1)} %get-tuple-element.60.refs_9_, bf16[3072,768]{1,0:T(8,128)(2,1)S(1)} %copy-done.1), kind=kOutput, calls=%fused_computation.17 | convolution fusion | flops 4831838208 | bytes 12582912 | tf_op jit(solution)/shard_map/dot_general | solution.py:695
  21.7 0.0 copy-done.2
  21.7 0.0 copy-start.4
  21.7 0.0 copy-start.3
  21.7 10.5 %fusion.7 = (f32[1024,3072]{1,0:T(8,128)}, f32[1024,3072]{1,0:T(8,128)S(1)}) fusion(bf16[1024,768]{1,0:T(8,128)(2,1)S(1)} %fusion.11.refs_2_, bf16[768,3072]{1,0:T(8,128)(2,1)S(1)} %copy-done.2), kind=kOutput, calls=%fused_computation.9 | convolution fusion | flops 4857004032 | bytes 31457280 | tf_op jit(solution)/shard_map/dot_general | solution.py:696
  32.2 0.0 copy-done.4
  32.2 0.0 copy-done.3
  32.2 8.1 %fusion.8 = f32[3072,768]{1,0:T(8,128)} fusion(bf16[1024,768]{1,0:T(8,128)(2,1)S(1)} %copy-done.3, f32[1024,3072]{1,0:T(8,128)S(1)} %get-tuple-element.62), kind=kOutput, calls=%fused_computation.14 | convolution fusion | flops 4847566848 | bytes 23592960 | tf_op jit(solution)/shard_map/dot_general | solution.py:678
  40.3 167.9 %reduce_update_gather.1 = (bf16[4,4,4,4,2,24,768]{6,5,4,3,2,1,0:T(8,128)(2,1)}, f32[3,2,6,3072]{3,2,1,0:T(8,128)}, f32[3,2,24,768]{3,2,1,0:T(8,128)}, f32[8,128]...) custom-call(f32[4,4,4,2,24,768]{5,4,3,2,1,0:T(8,128)} %bitcast.19, ...), custom_call_target="tpu_custom_call" | custom-call | tf_op jit(solution)/shard_map/reduce_update_gather/pallas_call | solution.py:651
  208.2 15.5 %place_outputs.1 = (bf16[4,4,2,24,3072]{4,3,2,1,0:T(8,128)(2,1)}, bf16[4,4,2,2,2,24,768]{6,5,4,3,2,1,0:T(8,128)(2,1)}, bf16[4,4,2,24,3072]{4,3,2,1,0:T(8,128)(2,...) custom-call(bf16[4,4,4,2,2,2,24,768]{7,6,5,4,3,2,1,0:T(8,128)(2,1)} , ...), custom_call_target="tpu_custom_call" | custom-call | tf_op jit(solution)/shard_map/place_outputs/pallas_call | solution.py:661
Async XLA Ops:
  1.9 14.7 %copy-start.1 = (bf16[3072,768]{1,0:T(8,128)(2,1)S(1)}, bf16[3072,768]{1,0:T(8,128)(2,1)}, u32[]{:S(2)}) copy-start(bf16[3072,768]{1,0:T(8,128)(2,1)} %refs_4_.1) | copy-start | bytes 14155780
  14.0 2.7 %copy-start = (bf16[1024,3072]{1,0:T(8,128)(2,1)}, bf16[1024,3072]{1,0:T(8,128)(2,1)S(1)}, u32[]{:S(2)}) copy-start(bf16[1024,3072]{1,0:T(8,128)(2,1)S(1)} %get-tuple-element.60.refs_9_) | copy-start | bytes 18874372
  16.7 5.0 %copy-start.2 = (bf16[768,3072]{1,0:T(8,128)(2,1)S(1)}, bf16[768,3072]{1,0:T(8,128)(2,1)}, u32[]{:S(2)}) copy-start(bf16[768,3072]{1,0:T(8,128)(2,1)} %refs_5_.1) | copy-start | bytes 14155780
  21.7 10.5 %copy-start.4 = (bf16[1024,768]{1,0:T(8,128)(2,1)}, bf16[1024,768]{1,0:T(8,128)(2,1)S(1)}, u32[]{:S(2)}) copy-start(bf16[1024,768]{1,0:T(8,128)(2,1)S(1)} %fusion.11.refs_2_) | copy-start | bytes 4718596
  21.7 10.5 %copy-start.3 = (bf16[1024,768]{1,0:T(8,128)(2,1)S(1)}, bf16[1024,768]{1,0:T(8,128)(2,1)}, u32[]{:S(2)}) copy-start(bf16[1024,768]{1,0:T(8,128)(2,1)} %refs_1_.1) | copy-start | bytes 4718596

commit v4 on v3

--- a/solution.py
+++ b/solution.py
@@ -31,6 +31,7 @@
 COLOURS = 3
 SIDES = 2
 ALL = slice(None)
+WINDOW = 5
 TILE = 512
 
 
@@ -330,15 +331,15 @@
     end(row_loads)
     flipped[...] = mid_grad[...].T
     mid_acc[...] = jnp.zeros_like(mid_acc)
-    run(0, 2, fetch_a, store_a, work_a)
+    run(0, 1, fetch_a, store_a, work_a)
     pl.semaphore_wait(barrier, len(peers))
     pairs[DOWN2] = [remote(g_down2.at[:, :, :, 1 - core], peer_in.at[pair_slot[DOWN2]], pair_s.at[DOWN2, 0], pair_r.at[DOWN2, 0], partner)]
     pairs[DOWN2][0].start()
-    run(2, 5, fetch_a, store_a, work_a)
+    run(1, 4, fetch_a, store_a, work_a)
     issue_up(UP2, 0)
     add_pair(DOWN2)
     first[DOWN2].start()
-    run(5, tiles, fetch_a, store_a, work_a)
+    run(4, tiles, fetch_a, store_a, work_a)
     issue_up(UP2, 1)
     begin(fetch_b(0, 0) + fetch_c(0, 0))
     in_load = pltpu.make_async_copy(in_rows, left, row_sem.at[0])
@@ -550,9 +551,9 @@
     gathers[UP, EARLY].finish_direct()
     keeps[UP].wait()
     gathers[UP, MIDDLE].start_direct()
+    gathers[DOWN, LAST].forward()
     gathers[UP, MIDDLE].finish_direct()
     gathers[UP, LAST].start()
-    gathers[DOWN, LAST].forward()
     gathers[DOWN, LAST].finish()
     gathers[UP, LAST].forward()
     gathers[UP, LAST].finish()
@@ -573,9 +574,9 @@
     weights, states, norm_out, (w_tmp, up_tmp, down_tmp, in_sem, state_in, out_sem, state_out) = refs[:4], refs[4:16], refs[16], refs[17:]
     norm_out[0] = jnp.max(norm_ref[...])
     loads = [[pltpu.make_async_copy(w_ref.at[mat % SIDES * 2 + mat // SIDES, z], w_tmp.at[mat, z], in_sem.at[mat, z]) for z in range(SIDE)] for mat in range(SIDE)]
-    for row in loads:
-        for copy in row:
-            copy.start()
+    queue = [copy for row in loads for copy in row]
+    for copy in queue[:WINDOW]:
+        copy.start()
     state_loads = [pltpu.make_async_copy(up_ref, up_tmp, state_in.at[0]), pltpu.make_async_copy(down_ref, down_tmp, state_in.at[1])]
     for copy in state_loads:
         copy.start()
@@ -583,6 +584,9 @@
     for mat in range(SIDE):
         for z in range(SIDE):
             loads[mat][z].wait()
+            ahead = 4 * mat + z + WINDOW
+            if ahead < len(queue):
+                queue[ahead].start()
             if mat % SIDES:
                 copies = [pltpu.make_async_copy(w_tmp.at[mat, z], weights[mat].at[z], out_sem.at[mat, z, 0])]
             else:

time: 224 us -> 223 us (level)
    pallas_call x1, Pallas kernels: 168 us -> 165 us  [comm_call(): pl.pallas_call(functools.partial(comm_kernel, lanes), name='reduce_update...]
where the time goes in v4:
time: 223 us; the launch traced here: 222 us
  Pallas kernels  182 us (82%)
  matrix products  35.7 us (16%)
  local copies, waits for them, and re-layouts  2.67 us (1%)
    pallas_call x1, Pallas kernels, comm_call(): pl.pallas_call(functools.partial(comm_kernel, lanes), name='reduce_update...  165 us
    pallas_call x1, Pallas kernels, comm_call(): pl.pallas_call(functools.partial(place_kernel, lanes), name='place_output...  16.2 us
    dot_general x1, matrix products, shard_body(): jnp.dot(act_in, w_up1, preferred_element_type=jnp.float32)  12 us
    dot_general x1, matrix products, shard_body(): jnp.dot(mid_act, w_up2, preferred_element_type=jnp.float32)  10.5 us
    dot_general x1, matrix products, mat_tn(): lax.dot_general(left, right, (((0,), (0,)), ((), ())), preferred_element_...  8.14 us
    dot_general x1, matrix products, shard_body(): jnp.dot(act_up1, w_down1, preferred_element_type=jnp.float32)  5.02 us

profile of v4, /device:TPU:1, one launch (start us, length us, event | category | flops | bytes accessed | tf_op | source)
XLA Modules:
  0.0 222.2 jit_solution(3997305743045280731)
XLA Ops:
  1.9 0.0 copy-start.1
  2.0 12.0 %fusion.3 = (f32[1024,3072]{1,0:T(8,128)}, bf16[1024,3072]{1,0:T(8,128)(2,1)S(1)}) fusion(bf16[1024,768]{1,0:T(8,128)(2,1)} %refs_3_.1, bf16[768,3072]{1,0:T(8,128)(2,1)} %param.22), kind=kOutput, calls=%fused_computation.5 | convolution fusion | flops 4863295488 | bytes 25165824 | tf_op jit(solution)/shard_map/dot_general | solution.py:697
  14.0 0.0 copy-start
  14.0 2.6 %copy-done = bf16[1024,3072]{1,0:T(8,128)(2,1)} copy-done((bf16[1024,3072]{1,0:T(8,128)(2,1)}, bf16[1024,3072]{1,0:T(8,128)(2,1)S(1)}, u32[]{:S(2)}) %copy-start) | copy-done | bytes 6291480
  16.7 0.0 copy-done.1
  16.7 0.0 copy-start.2
  16.7 5.0 %fusion.11.refs_2_ = bf16[1024,768]{1,0:T(8,128)(2,1)S(1)} fusion(bf16[1024,3072]{1,0:T(8,128)(2,1)S(1)} %get-tuple-element.60.refs_9_, bf16[3072,768]{1,0:T(8,128)(2,1)S(1)} %copy-done.1), kind=kOutput, calls=%fused_computation.17 | convolution fusion | flops 4831838208 | bytes 12582912 | tf_op jit(solution)/shard_map/dot_general | solution.py:699
  21.7 0.0 copy-done.2
  21.7 0.0 copy-start.4
  21.7 0.0 copy-start.3
  21.7 10.5 %fusion.7 = (f32[1024,3072]{1,0:T(8,128)}, f32[1024,3072]{1,0:T(8,128)S(1)}) fusion(bf16[1024,768]{1,0:T(8,128)(2,1)S(1)} %fusion.11.refs_2_, bf16[768,3072]{1,0:T(8,128)(2,1)S(1)} %copy-done.2), kind=kOutput, calls=%fused_computation.9 | convolution fusion | flops 4857004032 | bytes 31457280 | tf_op jit(solution)/shard_map/dot_general | solution.py:700
  32.2 0.0 copy-done.4
  32.2 0.0 copy-done.3
  32.2 8.1 %fusion.8 = f32[3072,768]{1,0:T(8,128)} fusion(bf16[1024,768]{1,0:T(8,128)(2,1)S(1)} %copy-done.3, f32[1024,3072]{1,0:T(8,128)S(1)} %get-tuple-element.62), kind=kOutput, calls=%fused_computation.14 | convolution fusion | flops 4847566848 | bytes 23592960 | tf_op jit(solution)/shard_map/dot_general | solution.py:682
  40.3 165.5 %reduce_update_gather.1 = (bf16[4,4,4,4,2,24,768]{6,5,4,3,2,1,0:T(8,128)(2,1)}, f32[3,2,6,3072]{3,2,1,0:T(8,128)}, f32[3,2,24,768]{3,2,1,0:T(8,128)}, f32[8,128]...) custom-call(f32[4,4,4,2,24,768]{5,4,3,2,1,0:T(8,128)} %bitcast.19, ...), custom_call_target="tpu_custom_call" | custom-call | tf_op jit(solution)/shard_map/reduce_update_gather/pallas_call | solution.py:655
  205.8 16.2 %place_outputs.1 = (bf16[4,4,2,24,3072]{4,3,2,1,0:T(8,128)(2,1)}, bf16[4,4,2,2,2,24,768]{6,5,4,3,2,1,0:T(8,128)(2,1)}, bf16[4,4,2,24,3072]{4,3,2,1,0:T(8,128)(2,...) custom-call(bf16[4,4,4,2,2,2,24,768]{7,6,5,4,3,2,1,0:T(8,128)(2,1)} , ...), custom_call_target="tpu_custom_call" | custom-call | tf_op jit(solution)/shard_map/place_outputs/pallas_call | solution.py:665
Async XLA Ops:
  1.9 14.7 %copy-start.1 = (bf16[3072,768]{1,0:T(8,128)(2,1)S(1)}, bf16[3072,768]{1,0:T(8,128)(2,1)}, u32[]{:S(2)}) copy-start(bf16[3072,768]{1,0:T(8,128)(2,1)} %refs_4_.1) | copy-start | bytes 14155780
  14.0 2.7 %copy-start = (bf16[1024,3072]{1,0:T(8,128)(2,1)}, bf16[1024,3072]{1,0:T(8,128)(2,1)S(1)}, u32[]{:S(2)}) copy-start(bf16[1024,3072]{1,0:T(8,128)(2,1)S(1)} %get-tuple-element.60.refs_9_) | copy-start | bytes 18874372
  16.7 5.0 %copy-start.2 = (bf16[768,3072]{1,0:T(8,128)(2,1)S(1)}, bf16[768,3072]{1,0:T(8,128)(2,1)}, u32[]{:S(2)}) copy-start(bf16[768,3072]{1,0:T(8,128)(2,1)} %refs_5_.1) | copy-start | bytes 14155780
  21.7 10.5 %copy-start.4 = (bf16[1024,768]{1,0:T(8,128)(2,1)}, bf16[1024,768]{1,0:T(8,128)(2,1)S(1)}, u32[]{:S(2)}) copy-start(bf16[1024,768]{1,0:T(8,128)(2,1)S(1)} %fusion.11.refs_2_) | copy-start | bytes 4718596
  21.7 10.5 %copy-start.3 = (bf16[1024,768]{1,0:T(8,128)(2,1)S(1)}, bf16[1024,768]{1,0:T(8,128)(2,1)}, u32[]{:S(2)}) copy-start(bf16[1024,768]{1,0:T(8,128)(2,1)} %refs_1_.1) | copy-start | bytes 4718596

commit v5 on v4

--- a/solution.py
+++ b/solution.py
@@ -31,7 +31,7 @@
 COLOURS = 3
 SIDES = 2
 ALL = slice(None)
-WINDOW = 5
+WINDOW = 16
 TILE = 512
 
 
@@ -50,7 +50,7 @@
     (total, peer_in, rs1, rs2, rs3, norm_line, norm_plane, send_g, recv_g, send_w, recv_w, block_tmp, w_own, up_state, down_state), refs = refs[:15], refs[15:]
     (left, flipped, mid_acc, mid_grad, w_tile, act_tile, der_tile, out_tile), refs = refs[:8], refs[8:]
     (load_sem, state_sem, pair_s, pair_r, rs1_s, rs1_r, rs2_s, rs2_r, rs3_s, rs3_r, nc_s, nc_r, na_s, na_r, xg_s, xg_r, xw_s, xw_r, own_sem, ag_s, ag_r, out_s, out_r) = refs[:23]
-    row_sem, tile_sem, store_sem, pair_credit, ring_credit = refs[23:]
+    row_sem, tile_sem, store_sem, pair_credit, ring_credit, early_l, early_s, early_r = refs[23:]
     half = lanes // 2
     me = lax.axis_index("data")
     core = lax.rem(me, SIDES)
@@ -105,7 +105,18 @@
 
     loads[DOWN1] = [pltpu.make_async_copy(total.at[1], total.at[1], load_sem.at[DOWN1, 0])]
     pairs[DOWN1] = [remote(peer_in.at[pair_slot[DOWN1]], peer_in.at[pair_slot[DOWN1]], pair_s.at[DOWN1, 0], pair_r.at[DOWN1, 0], partner)]
-    loads[DOWN2] = [pltpu.make_async_copy(g_down2.at[:, :, :, core], total.at[3], load_sem.at[DOWN2, 0])]
+    early = {}
+    for hops in (2, 1, 3, 0):
+        for colour in range(COLOURS):
+            axis = ORDERS[colour][0]
+            where = [ALL] * 3
+            where[axis] = step(axis, hops)
+            rows = pl.ds(CHUNK * colour, CHUNK)
+            spots = (colour, hops)
+            early[spots] = (
+                pltpu.make_async_copy(g_down2.at[(*where, core, rows)], total.at[(DOWN2, *where, rows)], early_l.at[spots]),
+                remote(g_down2.at[(*where, 1 - core, rows)], peer_in.at[(pair_slot[DOWN2], *where, rows)], early_s.at[spots], early_r.at[spots], partner),
+            )
 
     tiles = SIDE * lanes // TILE
 
@@ -139,7 +150,7 @@
     row_loads = [pltpu.make_async_copy(grad_rows, left, row_sem.at[0]), pltpu.make_async_copy(mid_rows, mid_grad, row_sem.at[1])]
     begin(row_loads)
     begin(fetch_a(0, 0))
-    begin(loads[DOWN2])
+    begin([copies[0] for copies in early.values()])
     state_loads = []
     for field in range(COLOURS):
         for mat in range(SIDE):
@@ -230,8 +241,8 @@
             coord = step(axis, 1 if side == 0 else 3)
             return coord, device(axis, coord)
 
-        def start(self):
-            for kind in range(SIDES):
+        def start(self, kinds=(0, 1)):
+            for kind in kinds:
                 for colour in range(COLOURS):
                     for side in range(SIDES):
                         coord, target = self.near(colour, side)
@@ -315,8 +326,22 @@
             return carry
 
         lax.fori_loop(0, 16, add, 0)
-        if mat >= 2:
+        if mat == UP2:
             pl.semaphore_signal(pair_credit, device_id=(partner,), device_id_type=MESH)
+
+    def add_early(hops):
+        for colour in range(COLOURS):
+            early[colour, hops][0].wait()
+            early[colour, hops][1].wait_recv()
+            axis = ORDERS[colour][0]
+
+            def add(i, carry, colour=colour, axis=axis):
+                coords = {axis: step(axis, hops), (1 if axis == 0 else 0): i}
+                own = part(DOWN2, coords, colour, None)
+                total[own] = total[own] + peer_in[part(pair_slot[DOWN2], coords, colour, None)]
+                return carry
+
+            lax.fori_loop(0, 4, add, 0)
 
     ring = [device(axis, step(axis, hops)) for axis in range(COLOURS) for hops in (1, 3)]
 
@@ -333,12 +358,19 @@
     mid_acc[...] = jnp.zeros_like(mid_acc)
     run(0, 1, fetch_a, store_a, work_a)
     pl.semaphore_wait(barrier, len(peers))
-    pairs[DOWN2] = [remote(g_down2.at[:, :, :, 1 - core], peer_in.at[pair_slot[DOWN2]], pair_s.at[DOWN2, 0], pair_r.at[DOWN2, 0], partner)]
-    pairs[DOWN2][0].start()
-    run(1, 4, fetch_a, store_a, work_a)
+    pairs[DOWN2] = [copies[1] for copies in early.values()]
+    begin(pairs[DOWN2])
+    run(1, 2, fetch_a, store_a, work_a)
+    add_early(2)
+    first[DOWN2].start((FAR,))
+    run(2, 4, fetch_a, store_a, work_a)
     issue_up(UP2, 0)
-    add_pair(DOWN2)
-    first[DOWN2].start()
+    add_early(1)
+    add_early(3)
+    first[DOWN2].start((NEAR,))
+    add_early(0)
+    pl.semaphore_signal(pair_credit, device_id=(partner,), device_id_type=MESH)
+    first[DOWN2].forward()
     run(4, tiles, fetch_a, store_a, work_a)
     issue_up(UP2, 1)
     begin(fetch_b(0, 0) + fetch_c(0, 0))
@@ -346,7 +378,6 @@
     in_load.start()
     mid_grad[...] = mid_acc[...].reshape(mid_grad.shape).astype(jnp.bfloat16)
     run(0, 3, fetch_b, store_b, work_b)
-    first[DOWN2].forward()
     add_pair(UP2)
     first[UP2].start()
     run(3, tiles, fetch_b, store_b, work_b)
@@ -650,7 +681,7 @@
         dma((SIDE, COLOURS, SIDES, COLOURS)), dma((SIDE, COLOURS, SIDES, COLOURS)), dma((SIDES, COLOURS, SIDES, COLOURS)), dma((SIDES, COLOURS, SIDES, COLOURS)), dma((SIDES, COLOURS, COLOURS)), dma((SIDES, COLOURS, COLOURS)),
         dma((7,)), dma((7,)), dma((15,)), dma((15,)), dma((COLOURS,)), dma((COLOURS,)), dma((COLOURS,)), dma((COLOURS,)),
         dma((SIDES,)), dma((SIDES, COLOURS, COLOURS, SIDES, COLOURS)), dma((SIDES, COLOURS, COLOURS, SIDES, COLOURS)), dma((SIDES, 15)), dma((SIDES, 15)),
-        dma((SIDES,)), dma((SIDES, COLOURS)), dma((SIDES,)), pltpu.SemaphoreType.REGULAR, pltpu.SemaphoreType.REGULAR((2,)),
+        dma((SIDES,)), dma((SIDES, COLOURS)), dma((SIDES,)), pltpu.SemaphoreType.REGULAR, pltpu.SemaphoreType.REGULAR((2,)), dma((COLOURS, SIDE)), dma((COLOURS, SIDE)), dma((COLOURS, SIDE)),
     ]
     outs = pl.pallas_call(
         functools.partial(comm_kernel, lanes),

time: 223 us -> 221 us (level)
  no operation moved by 1% of the time
where the time goes in v5:
time: 221 us; the launch traced here: 220 us
  Pallas kernels  180 us (81%)
  matrix products  35.7 us (16%)
  local copies, waits for them, and re-layouts  2.67 us (1%)
    pallas_call x1, Pallas kernels, comm_call(): pl.pallas_call(functools.partial(comm_kernel, lanes), name='reduce_update...  164 us
    pallas_call x1, Pallas kernels, comm_call(): pl.pallas_call(functools.partial(place_kernel, lanes), name='place_output...  15.5 us
    dot_general x1, matrix products, shard_body(): jnp.dot(act_in, w_up1, preferred_element_type=jnp.float32)  12 us
    dot_general x1, matrix products, shard_body(): jnp.dot(mid_act, w_up2, preferred_element_type=jnp.float32)  10.5 us
    dot_general x1, matrix products, mat_tn(): lax.dot_general(left, right, (((0,), (0,)), ((), ())), preferred_element_...  8.14 us
    dot_general x1, matrix products, shard_body(): jnp.dot(act_up1, w_down1, preferred_element_type=jnp.float32)  5.02 us

profile of v5, /device:TPU:1, one launch (start us, length us, event | category | flops | bytes accessed | tf_op | source)
XLA Modules:
  0.0 220.4 jit_solution(12690641797341329744)
XLA Ops:
  1.9 0.0 copy-start.1
  2.0 12.0 %fusion.3 = (f32[1024,3072]{1,0:T(8,128)}, bf16[1024,3072]{1,0:T(8,128)(2,1)S(1)}) fusion(bf16[1024,768]{1,0:T(8,128)(2,1)} %refs_3_.1, bf16[768,3072]{1,0:T(8,128)(2,1)} %param.22), kind=kOutput, calls=%fused_computation.5 | convolution fusion | flops 4863295488 | bytes 25165824 | tf_op jit(solution)/shard_map/dot_general | solution.py:728
  14.0 0.0 copy-start
  14.0 2.6 %copy-done = bf16[1024,3072]{1,0:T(8,128)(2,1)} copy-done((bf16[1024,3072]{1,0:T(8,128)(2,1)}, bf16[1024,3072]{1,0:T(8,128)(2,1)S(1)}, u32[]{:S(2)}) %copy-start) | copy-done | bytes 6291480
  16.7 0.0 copy-done.1
  16.7 0.0 copy-start.2
  16.7 5.0 %fusion.11.refs_2_ = bf16[1024,768]{1,0:T(8,128)(2,1)S(1)} fusion(bf16[1024,3072]{1,0:T(8,128)(2,1)S(1)} %get-tuple-element.60.refs_9_, bf16[3072,768]{1,0:T(8,128)(2,1)S(1)} %copy-done.1), kind=kOutput, calls=%fused_computation.17 | convolution fusion | flops 4831838208 | bytes 12582912 | tf_op jit(solution)/shard_map/dot_general | solution.py:730
  21.7 0.0 copy-done.2
  21.7 0.0 copy-start.4
  21.7 0.0 copy-start.3
  21.7 10.5 %fusion.7 = (f32[1024,3072]{1,0:T(8,128)}, f32[1024,3072]{1,0:T(8,128)S(1)}) fusion(bf16[1024,768]{1,0:T(8,128)(2,1)S(1)} %fusion.11.refs_2_, bf16[768,3072]{1,0:T(8,128)(2,1)S(1)} %copy-done.2), kind=kOutput, calls=%fused_computation.9 | convolution fusion | flops 4857004032 | bytes 31457280 | tf_op jit(solution)/shard_map/dot_general | solution.py:731
  32.2 0.0 copy-done.4
  32.2 0.0 copy-done.3
  32.2 8.1 %fusion.8 = f32[3072,768]{1,0:T(8,128)} fusion(bf16[1024,768]{1,0:T(8,128)(2,1)S(1)} %copy-done.3, f32[1024,3072]{1,0:T(8,128)S(1)} %get-tuple-element.62), kind=kOutput, calls=%fused_computation.14 | convolution fusion | flops 4847566848 | bytes 23592960 | tf_op jit(solution)/shard_map/dot_general | solution.py:713
  40.3 164.3 %reduce_update_gather.1 = (bf16[4,4,4,4,2,24,768]{6,5,4,3,2,1,0:T(8,128)(2,1)}, f32[3,2,6,3072]{3,2,1,0:T(8,128)}, f32[3,2,24,768]{3,2,1,0:T(8,128)}, f32[8,128]...) custom-call(f32[4,4,4,2,24,768]{5,4,3,2,1,0:T(8,128)} %bitcast.19, ...), custom_call_target="tpu_custom_call" | custom-call | tf_op jit(solution)/shard_map/reduce_update_gather/pallas_call | solution.py:686
  204.7 15.5 %place_outputs.1 = (bf16[4,4,2,24,3072]{4,3,2,1,0:T(8,128)(2,1)}, bf16[4,4,2,2,2,24,768]{6,5,4,3,2,1,0:T(8,128)(2,1)}, bf16[4,4,2,24,3072]{4,3,2,1,0:T(8,128)(2,...) custom-call(bf16[4,4,4,2,2,2,24,768]{7,6,5,4,3,2,1,0:T(8,128)(2,1)} , ...), custom_call_target="tpu_custom_call" | custom-call | tf_op jit(solution)/shard_map/place_outputs/pallas_call | solution.py:696
Async XLA Ops:
  1.9 14.7 %copy-start.1 = (bf16[3072,768]{1,0:T(8,128)(2,1)S(1)}, bf16[3072,768]{1,0:T(8,128)(2,1)}, u32[]{:S(2)}) copy-start(bf16[3072,768]{1,0:T(8,128)(2,1)} %refs_4_.1) | copy-start | bytes 14155780
  14.0 2.7 %copy-start = (bf16[1024,3072]{1,0:T(8,128)(2,1)}, bf16[1024,3072]{1,0:T(8,128)(2,1)S(1)}, u32[]{:S(2)}) copy-start(bf16[1024,3072]{1,0:T(8,128)(2,1)S(1)} %get-tuple-element.60.refs_9_) | copy-start | bytes 18874372
  16.7 5.0 %copy-start.2 = (bf16[768,3072]{1,0:T(8,128)(2,1)S(1)}, bf16[768,3072]{1,0:T(8,128)(2,1)}, u32[]{:S(2)}) copy-start(bf16[768,3072]{1,0:T(8,128)(2,1)} %refs_5_.1) | copy-start | bytes 14155780
  21.7 10.5 %copy-start.4 = (bf16[1024,768]{1,0:T(8,128)(2,1)}, bf16[1024,768]{1,0:T(8,128)(2,1)S(1)}, u32[]{:S(2)}) copy-start(bf16[1024,768]{1,0:T(8,128)(2,1)S(1)} %fusion.11.refs_2_) | copy-start | bytes 4718596
  21.7 10.5 %copy-start.3 = (bf16[1024,768]{1,0:T(8,128)(2,1)S(1)}, bf16[1024,768]{1,0:T(8,128)(2,1)}, u32[]{:S(2)}) copy-start(bf16[1024,768]{1,0:T(8,128)(2,1)} %refs_1_.1) | copy-start | bytes 4718596

commit v6 on v5

--- a/solution.py
+++ b/solution.py
@@ -377,17 +377,18 @@
     in_load = pltpu.make_async_copy(in_rows, left, row_sem.at[0])
     in_load.start()
     mid_grad[...] = mid_acc[...].reshape(mid_grad.shape).astype(jnp.bfloat16)
-    run(0, 3, fetch_b, store_b, work_b)
+    run(0, 2, fetch_b, store_b, work_b)
     add_pair(UP2)
     first[UP2].start()
-    run(3, tiles, fetch_b, store_b, work_b)
+    close(DOWN2)
+    run(2, tiles, fetch_b, store_b, work_b)
     pl.semaphore_wait(pair_credit)
     issue_rows(0, 64)
     in_load.wait()
     flipped[...] = left[...].T
-    run(0, 3, fetch_c, store_c, work_c)
-    close(DOWN2)
+    run(0, 1, fetch_c, store_c, work_c)
     first[UP2].forward()
+    run(1, 3, fetch_c, store_c, work_c)
     pl.semaphore_wait(pair_credit)
     issue_up(UP1, 0)
     add_pair(DOWN1)

time: 221 us -> 216 us (0.977)
  Pallas kernels: 180 us -> 175 us
    pallas_call x1, Pallas kernels: 164 us -> 160 us  [comm_call(): pl.pallas_call(functools.partial(comm_kernel, lanes), name='reduce_update...]
where the time goes in v6:
time: 216 us
  Pallas kernels  175 us (81%)
  matrix products  35.7 us (17%)
  local copies, waits for them, and re-layouts  2.67 us (1%)
  between operations  2.18 us (1%)
    pallas_call x1, Pallas kernels, comm_call(): pl.pallas_call(functools.partial(comm_kernel, lanes), name='reduce_update...  160 us
    pallas_call x1, Pallas kernels, comm_call(): pl.pallas_call(functools.partial(place_kernel, lanes), name='place_output...  15.5 us
    dot_general x1, matrix products, shard_body(): jnp.dot(act_in, w_up1, preferred_element_type=jnp.float32)  12 us
    dot_general x1, matrix products, shard_body(): jnp.dot(mid_act, w_up2, preferred_element_type=jnp.float32)  10.5 us
    dot_general x1, matrix products, mat_tn(): lax.dot_general(left, right, (((0,), (0,)), ((), ())), preferred_element_...  8.14 us
    dot_general x1, matrix products, shard_body(): jnp.dot(act_up1, w_down1, preferred_element_type=jnp.float32)  5.02 us

profile of v6, /device:TPU:1, one launch (start us, length us, event | category | flops | bytes accessed | tf_op | source)
XLA Modules:
  0.0 216.0 jit_solution(5184675343868000970)
XLA Ops:
  1.9 0.0 copy-start.1
  2.0 12.0 %fusion.3 = (f32[1024,3072]{1,0:T(8,128)}, bf16[1024,3072]{1,0:T(8,128)(2,1)S(1)}) fusion(bf16[1024,768]{1,0:T(8,128)(2,1)} %refs_3_.1, bf16[768,3072]{1,0:T(8,128)(2,1)} %param.22), kind=kOutput, calls=%fused_computation.5 | convolution fusion | flops 4863295488 | bytes 25165824 | tf_op jit(solution)/shard_map/dot_general | solution.py:729
  14.0 0.0 copy-start
  14.0 2.6 %copy-done = bf16[1024,3072]{1,0:T(8,128)(2,1)} copy-done((bf16[1024,3072]{1,0:T(8,128)(2,1)}, bf16[1024,3072]{1,0:T(8,128)(2,1)S(1)}, u32[]{:S(2)}) %copy-start) | copy-done | bytes 6291480
  16.7 0.0 copy-done.1
  16.7 0.0 copy-start.2
  16.7 5.0 %fusion.11.refs_2_ = bf16[1024,768]{1,0:T(8,128)(2,1)S(1)} fusion(bf16[1024,3072]{1,0:T(8,128)(2,1)S(1)} %get-tuple-element.60.refs_9_, bf16[3072,768]{1,0:T(8,128)(2,1)S(1)} %copy-done.1), kind=kOutput, calls=%fused_computation.17 | convolution fusion | flops 4831838208 | bytes 12582912 | tf_op jit(solution)/shard_map/dot_general | solution.py:731
  21.7 0.0 copy-done.2
  21.7 0.0 copy-start.4
  21.7 0.0 copy-start.3
  21.7 10.5 %fusion.7 = (f32[1024,3072]{1,0:T(8,128)}, f32[1024,3072]{1,0:T(8,128)S(1)}) fusion(bf16[1024,768]{1,0:T(8,128)(2,1)S(1)} %fusion.11.refs_2_, bf16[768,3072]{1,0:T(8,128)(2,1)S(1)} %copy-done.2), kind=kOutput, calls=%fused_computation.9 | convolution fusion | flops 4857004032 | bytes 31457280 | tf_op jit(solution)/shard_map/dot_general | solution.py:732
  32.2 0.0 copy-done.4
  32.2 0.0 copy-done.3
  32.2 8.1 %fusion.8 = f32[3072,768]{1,0:T(8,128)} fusion(bf16[1024,768]{1,0:T(8,128)(2,1)S(1)} %copy-done.3, f32[1024,3072]{1,0:T(8,128)S(1)} %get-tuple-element.62), kind=kOutput, calls=%fused_computation.14 | convolution fusion | flops 4847566848 | bytes 23592960 | tf_op jit(solution)/shard_map/dot_general | solution.py:714
  40.3 159.9 %reduce_update_gather.1 = (bf16[4,4,4,4,2,24,768]{6,5,4,3,2,1,0:T(8,128)(2,1)}, f32[3,2,6,3072]{3,2,1,0:T(8,128)}, f32[3,2,24,768]{3,2,1,0:T(8,128)}, f32[8,128]...) custom-call(f32[4,4,4,2,24,768]{5,4,3,2,1,0:T(8,128)} %bitcast.19, ...), custom_call_target="tpu_custom_call" | custom-call | tf_op jit(solution)/shard_map/reduce_update_gather/pallas_call | solution.py:687
  200.3 15.5 %place_outputs.1 = (bf16[4,4,2,24,3072]{4,3,2,1,0:T(8,128)(2,1)}, bf16[4,4,2,2,2,24,768]{6,5,4,3,2,1,0:T(8,128)(2,1)}, bf16[4,4,2,24,3072]{4,3,2,1,0:T(8,128)(2,...) custom-call(bf16[4,4,4,2,2,2,24,768]{7,6,5,4,3,2,1,0:T(8,128)(2,1)} , ...), custom_call_target="tpu_custom_call" | custom-call | tf_op jit(solution)/shard_map/place_outputs/pallas_call | solution.py:697
Async XLA Ops:
  1.9 14.7 %copy-start.1 = (bf16[3072,768]{1,0:T(8,128)(2,1)S(1)}, bf16[3072,768]{1,0:T(8,128)(2,1)}, u32[]{:S(2)}) copy-start(bf16[3072,768]{1,0:T(8,128)(2,1)} %refs_4_.1) | copy-start | bytes 14155780
  14.0 2.7 %copy-start = (bf16[1024,3072]{1,0:T(8,128)(2,1)}, bf16[1024,3072]{1,0:T(8,128)(2,1)S(1)}, u32[]{:S(2)}) copy-start(bf16[1024,3072]{1,0:T(8,128)(2,1)S(1)} %get-tuple-element.60.refs_9_) | copy-start | bytes 18874372
  16.7 5.0 %copy-start.2 = (bf16[768,3072]{1,0:T(8,128)(2,1)S(1)}, bf16[768,3072]{1,0:T(8,128)(2,1)}, u32[]{:S(2)}) copy-start(bf16[768,3072]{1,0:T(8,128)(2,1)} %refs_5_.1) | copy-start | bytes 14155780
  21.7 10.5 %copy-start.4 = (bf16[1024,768]{1,0:T(8,128)(2,1)}, bf16[1024,768]{1,0:T(8,128)(2,1)S(1)}, u32[]{:S(2)}) copy-start(bf16[1024,768]{1,0:T(8,128)(2,1)S(1)} %fusion.11.refs_2_) | copy-start | bytes 4718596
  21.7 10.5 %copy-start.3 = (bf16[1024,768]{1,0:T(8,128)(2,1)S(1)}, bf16[1024,768]{1,0:T(8,128)(2,1)}, u32[]{:S(2)}) copy-start(bf16[1024,768]{1,0:T(8,128)(2,1)} %refs_1_.1) | copy-start | bytes 4718596
